TPU v7x, 32 devices: a whole 2x2x4 slice. The times are simulated.
32 devices in a mesh: fsdp: 32 (over z, y, x, core).
Axes of the slice: x: 2, y: 2, z: 4, core: 2. Of those that a mesh axis runs over, the one named last changes fastest.
Arguments:
- tokens: bfloat16 [32768, 768], P('fsdp'), may hold values from -80 to 80
- segment_ids: int32 [32768], P('fsdp'), may hold values from 0 to 20, as said below
- pad_mask: int32 [32768], P('fsdp'), may hold values from 0 to 1, as said below
- w_qkv: bfloat16 [768, 2304], P('fsdp'), may hold values from -0.25 to 0.25
- bias_query: bfloat16 [768], P('fsdp'), may hold values from -3 to 3
- bias_value: bfloat16 [768], P('fsdp'), may hold values from -3 to 3
- w_out: bfloat16 [768, 768], P('fsdp'), may hold values from -1.25 to 1.25
- bias_out: bfloat16 [768], P('fsdp'), may hold values from -3 to 3
- gain_one: bfloat16 [768], P('fsdp'), may hold values from 0.25 to 1.75
- shift_one: bfloat16 [768], P('fsdp'), may hold values from -3 to 3
- w_up: bfloat16 [768, 3072], P('fsdp'), may hold values from -0.21875 to 0.21875
- bias_up: bfloat16 [3072], P('fsdp'), may hold values from -3 to 3
- w_down: bfloat16 [3072, 768], P('fsdp'), may hold values from -0.109375 to 0.109375
- bias_down: bfloat16 [768], P('fsdp'), may hold values from -3 to 3
- gain_two: bfloat16 [768], P('fsdp'), may hold values from 0.25 to 1.75
- shift_two: bfloat16 [768], P('fsdp'), may hold values from -3 to 3
- cotangent: bfloat16 [32768, 768], P('fsdp'), may hold values from -6 to 6
Outputs:
- layer_out: bfloat16 [32768, 768], P('fsdp')
- grad_tokens: float32 [32768, 768], P('fsdp')
- grad_w_qkv: float32 [768, 2304], P('fsdp')
- grad_bias_query: float32 [768], P('fsdp')
- grad_bias_value: float32 [768], P('fsdp')
- grad_w_out: float32 [768, 768], P('fsdp')
- grad_bias_out: float32 [768], P('fsdp')
- grad_gain_one: float32 [768], P('fsdp')
- grad_shift_one: float32 [768], P('fsdp')
- grad_w_up: float32 [768, 3072], P('fsdp')
- grad_bias_up: float32 [3072], P('fsdp')
- grad_w_down: float32 [3072, 768], P('fsdp')
- grad_bias_down: float32 [768], P('fsdp')
- grad_gain_two: float32 [768], P('fsdp')
- grad_shift_two: float32 [768], P('fsdp')
Inputs may be any that keep to these rules, and one draw needn't show every extreme that they name: `segment_ids`: sequence numbers of the packed tokens, starting at 0 and never falling; there are exactly 21 sequences, each of 1024 to 2048 tokens, and one holds exactly 2048. `pad_mask`: the first token of every sequence is 1.
All inputs are finite; a program needn't handle non-finite values.
Results may differ from a plain program's by a relative error of at most 0.015.
The roundings to bfloat16 on the way count: a program that leaves them out, or rounds other values in their place, can miss the bound.
Values may be sent and summed in bfloat16 or wider, within the bound.
A program may use at most 320 MiB of HBM per device.

v0:
```python
import jax
import jax.numpy as jnp
from jax import lax
from jax.sharding import PartitionSpec as P

D = 768
HEADS = 12
HEAD_DIM = 64
LEN_MAX = 2048


eps_norm = 1e-12
score_scale = 0.125


def from_behind(block, axis, distance):
    devices = range(lax.axis_size(axis))
    route = [(i - distance, i) for i in devices if i - distance in devices]
    return lax.ppermute(block, axis, route)


def norm_rows(hidden, gain_row, shift_row):
    centre = hidden - jnp.mean(hidden, axis=-1, keepdims=True)
    spread = jnp.mean(centre * centre, axis=-1, keepdims=True)
    return centre * lax.rsqrt(spread + eps_norm) * gain_row + shift_row


def gelu_exact(pre_act):
    return 0.5 * pre_act * (1.0 + jax.scipy.special.erf(pre_act * 0.7071067811865476))


def split_heads(matrix):
    return matrix.reshape(matrix.shape[0], HEADS, HEAD_DIM).transpose(1, 0, 2)


def join_heads(stacked):
    return stacked.transpose(1, 0, 2).reshape(stacked.shape[1], HEADS * HEAD_DIM)


def head_scores(q_head, k_head, allowed):
    scores = (
        jnp.einsum("qd,kd->qk", q_head, k_head, preferred_element_type=jnp.float32) * score_scale
    )
    return jnp.where(allowed, scores, -jnp.inf)


def probs_inner(q_head, k_head, v_head, d_ctx, log_row, allowed):
    scores = head_scores(q_head, k_head, allowed)
    probs = jnp.exp(scores - log_row[:, None])
    d_probs = jnp.einsum("qd,kd->qk", d_ctx, v_head, preferred_element_type=jnp.float32)
    inner = jnp.sum(probs * d_probs, axis=-1, keepdims=True)
    return (probs, d_probs, inner)


def body(
    tokens,
    segment_ids,
    pad_mask,
    w_qkv,
    bias_query,
    bias_value,
    w_out,
    bias_out,
    gain_one,
    shift_one,
    w_up,
    bias_up,
    w_down,
    bias_down,
    gain_two,
    shift_two,
    cotangent,
):
    shards = (
        w_qkv,
        bias_query,
        bias_value,
        w_out,
        bias_out,
        gain_one,
        shift_one,
        w_up,
        bias_up,
        w_down,
        bias_down,
        gain_two,
        shift_two,
    )
    gathered = (
        lax.all_gather(shards[0], "fsdp", axis=0, tiled=True),
        lax.all_gather(shards[1], "fsdp", axis=0, tiled=True),
        lax.all_gather(shards[2], "fsdp", axis=0, tiled=True),
        lax.all_gather(shards[3], "fsdp", axis=0, tiled=True),
        lax.all_gather(shards[4], "fsdp", axis=0, tiled=True),
        lax.all_gather(shards[5], "fsdp", axis=0, tiled=True),
        lax.all_gather(shards[6], "fsdp", axis=0, tiled=True),
        lax.all_gather(shards[7], "fsdp", axis=0, tiled=True),
        lax.all_gather(shards[8], "fsdp", axis=0, tiled=True),
        lax.all_gather(shards[9], "fsdp", axis=0, tiled=True),
        lax.all_gather(shards[10], "fsdp", axis=0, tiled=True),
        lax.all_gather(shards[11], "fsdp", axis=0, tiled=True),
        lax.all_gather(shards[12], "fsdp", axis=0, tiled=True),
    )
    (
        wq_full,
        bq_full,
        bv_full,
        wo_full,
        bo_full,
        g1_full,
        s1_full,
        wu_full,
        bu_full,
        wd_full,
        bd_full,
        g2_full,
        s2_full,
    ) = gathered
    row_count = tokens.shape[0]
    device_reach = (LEN_MAX - 2) // row_count + 1
    mixed = jnp.dot(tokens, wq_full, preferred_element_type=jnp.float32)
    queries = (mixed[:, :D] + bq_full.astype(jnp.float32)).astype(jnp.bfloat16)
    key_vals = jnp.concatenate(
        [mixed[:, D : 2 * D], mixed[:, 2 * D :] + bv_full.astype(jnp.float32)], axis=1
    ).astype(jnp.bfloat16)
    own_tag = jnp.where(pad_mask == 1, segment_ids + 1, 0)
    query_tag = segment_ids + 1
    window_parts = []
    tag_parts = []
    for offset in range(-device_reach, device_reach + 1):
        if offset == 0:
            window_parts.append(key_vals)
            tag_parts.append(own_tag)
        else:
            got_vals, got_tag = from_behind((key_vals, own_tag), "fsdp", -offset)
            window_parts.append(got_vals)
            tag_parts.append(got_tag)
    window_kv = jnp.concatenate(window_parts, axis=0)
    window_tag = jnp.concatenate(tag_parts, axis=0)
    allowed = query_tag[:, None] == window_tag[None, :]
    q_heads = split_heads(queries)
    k_heads = split_heads(window_kv[:, :D])
    v_heads = split_heads(window_kv[:, D:])

    def head_forward(stacked):
        q_head, k_head, v_head = stacked
        scores = head_scores(q_head, k_head, allowed)
        top_score = jnp.max(scores, axis=-1, keepdims=True)
        exp_scores = jnp.exp(scores - top_score)
        total = jnp.sum(exp_scores, axis=-1, keepdims=True)
        probs_low = (exp_scores / total).astype(jnp.bfloat16)
        context = jnp.dot(probs_low, v_head, preferred_element_type=jnp.float32)
        return (context, (top_score + jnp.log(total))[:, 0])

    ctx_heads, log_total = lax.map(head_forward, (q_heads, k_heads, v_heads))
    context = join_heads(ctx_heads).astype(jnp.bfloat16)
    tokens_f = tokens.astype(jnp.float32)
    branch = jnp.dot(context, wo_full, preferred_element_type=jnp.float32) + bo_full.astype(
        jnp.float32
    )
    first, norm_one_back = jax.vjp(
        norm_rows, tokens_f + branch, g1_full.astype(jnp.float32), s1_full.astype(jnp.float32)
    )
    up_in = first.astype(jnp.bfloat16)
    pre_act = jnp.dot(up_in, wu_full, preferred_element_type=jnp.float32) + bu_full.astype(
        jnp.float32
    )
    gelu_val, gelu_back = jax.vjp(gelu_exact, pre_act)
    hidden = gelu_val.astype(jnp.bfloat16)
    ffn = jnp.dot(hidden, wd_full, preferred_element_type=jnp.float32) + bd_full.astype(jnp.float32)
    result, norm_two_back = jax.vjp(
        norm_rows, first + ffn, g2_full.astype(jnp.float32), s2_full.astype(jnp.float32)
    )
    layer_out = result.astype(jnp.bfloat16)
    wq_back, wo_back, wu_back, wd_back = (wq_full, wo_full, wu_full, wd_full)
    d_second, d_gain_two, d_shift_two = norm_two_back(cotangent.astype(jnp.float32))
    d_ffn = d_second.astype(jnp.bfloat16)
    d_bias_down = jnp.sum(d_ffn.astype(jnp.float32), axis=0)
    d_w_down = jnp.einsum("rf,rd->fd", hidden, d_ffn, preferred_element_type=jnp.float32)
    d_hidden = jnp.einsum("rd,fd->rf", d_ffn, wd_back, preferred_element_type=jnp.float32)
    d_pre = gelu_back(d_hidden)[0].astype(jnp.bfloat16)
    d_bias_up = jnp.sum(d_pre.astype(jnp.float32), axis=0)
    d_w_up = jnp.einsum("rd,rf->df", up_in, d_pre, preferred_element_type=jnp.float32)
    d_first = d_second + jnp.einsum("rf,df->rd", d_pre, wu_back, preferred_element_type=jnp.float32)
    d_mid, d_gain_one, d_shift_one = norm_one_back(d_first)
    d_branch = d_mid.astype(jnp.bfloat16)
    d_bias_out = jnp.sum(d_branch.astype(jnp.float32), axis=0)
    d_w_out = jnp.einsum("ri,ro->io", context, d_branch, preferred_element_type=jnp.float32)
    d_context = jnp.einsum(
        "ro,io->ri", d_branch, wo_back, preferred_element_type=jnp.float32
    ).astype(jnp.bfloat16)
    dc_heads = split_heads(d_context)

    def head_backward(stacked):
        q_head, k_head, v_head, d_ctx, log_row = stacked
        probs, d_probs, inner = probs_inner(q_head, k_head, v_head, d_ctx, log_row, allowed)
        d_values = jnp.einsum(
            "qk,qd->kd", probs.astype(jnp.bfloat16), d_ctx, preferred_element_type=jnp.float32
        )
        d_scores = (probs * (d_probs - inner)).astype(jnp.bfloat16)
        d_queries = jnp.dot(d_scores, k_head, preferred_element_type=jnp.float32) * score_scale
        d_keys = (
            jnp.einsum("qk,qd->kd", d_scores, q_head, preferred_element_type=jnp.float32)
            * score_scale
        )
        return (d_queries, d_keys, d_values)

    dq_heads, dk_heads, dv_heads = lax.map(
        head_backward, (q_heads, k_heads, v_heads, dc_heads, log_total)
    )
    window_grad = jnp.concatenate([join_heads(dk_heads), join_heads(dv_heads)], axis=1)
    own_grad = window_grad[device_reach * row_count : (device_reach + 1) * row_count]
    for offset in range(-device_reach, device_reach + 1):
        if offset != 0:
            block_grad = window_grad[
                (offset + device_reach) * row_count : (offset + device_reach + 1) * row_count
            ]
            own_grad = own_grad + from_behind(block_grad, "fsdp", offset)
    d_mixed = jnp.concatenate([join_heads(dq_heads), own_grad], axis=1).astype(jnp.bfloat16)
    d_mixed_f = d_mixed.astype(jnp.float32)
    d_bias_query = jnp.sum(d_mixed_f[:, :D], axis=0)
    d_bias_value = jnp.sum(d_mixed_f[:, 2 * D :], axis=0)
    d_w_qkv = jnp.einsum("rd,rc->dc", tokens, d_mixed, preferred_element_type=jnp.float32)
    grad_tokens = d_mid + jnp.einsum(
        "rc,dc->rd", d_mixed, wq_back, preferred_element_type=jnp.float32
    )
    owned = (
        lax.psum_scatter(d_w_qkv, "fsdp", scatter_dimension=0, tiled=True),
        lax.psum_scatter(d_bias_query, "fsdp", scatter_dimension=0, tiled=True),
        lax.psum_scatter(d_bias_value, "fsdp", scatter_dimension=0, tiled=True),
        lax.psum_scatter(d_w_out, "fsdp", scatter_dimension=0, tiled=True),
        lax.psum_scatter(d_bias_out, "fsdp", scatter_dimension=0, tiled=True),
        lax.psum_scatter(d_gain_one, "fsdp", scatter_dimension=0, tiled=True),
        lax.psum_scatter(d_shift_one, "fsdp", scatter_dimension=0, tiled=True),
        lax.psum_scatter(d_w_up, "fsdp", scatter_dimension=0, tiled=True),
        lax.psum_scatter(d_bias_up, "fsdp", scatter_dimension=0, tiled=True),
        lax.psum_scatter(d_w_down, "fsdp", scatter_dimension=0, tiled=True),
        lax.psum_scatter(d_bias_down, "fsdp", scatter_dimension=0, tiled=True),
        lax.psum_scatter(d_gain_two, "fsdp", scatter_dimension=0, tiled=True),
        lax.psum_scatter(d_shift_two, "fsdp", scatter_dimension=0, tiled=True),
    )
    return (
        layer_out,
        grad_tokens,
        owned[0],
        owned[1],
        owned[2],
        owned[3],
        owned[4],
        owned[5],
        owned[6],
        owned[7],
        owned[8],
        owned[9],
        owned[10],
        owned[11],
        owned[12],
    )


def solution(mesh):
    return jax.shard_map(
        body,
        mesh=mesh,
        in_specs=(
            P("fsdp", None),
            P("fsdp"),
            P("fsdp"),
            P("fsdp", None),
            P("fsdp"),
            P("fsdp"),
            P("fsdp", None),
            P("fsdp"),
            P("fsdp"),
            P("fsdp"),
            P("fsdp", None),
            P("fsdp"),
            P("fsdp", None),
            P("fsdp"),
            P("fsdp"),
            P("fsdp"),
            P("fsdp", None),
        ),
        out_specs=(
            P("fsdp", None),
            P("fsdp", None),
            P("fsdp", None),
            P("fsdp"),
            P("fsdp"),
            P("fsdp", None),
            P("fsdp"),
            P("fsdp"),
            P("fsdp"),
            P("fsdp", None),
            P("fsdp"),
            P("fsdp", None),
            P("fsdp"),
            P("fsdp"),
            P("fsdp"),
        ),
        check_vma=False,
    )
```

profile of v0, /device:TPU:0, one launch (start us, length us, event | category | flops | bytes accessed | tf_op | source)
XLA Modules:
  0.0 2136.3 jit_solution(12723488319502606294)
XLA Ops:
  17.0 42.5 %all-reduce.19 = (bf16[768]{0:T(1024)(128)(2,1)S(1)}, bf16[768]{0:T(1024)(128)(2,1)S(1)}, bf16[768]{0:T(1024)(128)(2,1)S(1)}, bf16[768]{0:T(1024)(128)(2,1)S(1)}...) all-reduce(bf16[768]{0:T(1024)(128)(2,1)S(1)} %dynamic-update-slice, ...), channel_id=1, replica_groups=mesh['fsdp'=32] {'fsdp'}, use_global_device_ids=true, to_apply=%add | all-reduce | flops 9216 | bytes 36864
  109.1 152.2 %collective-permute-done.4 = s32[1024]{0:T(1024)S(1)} collective-permute-done((s32[1024]{0:T(1024)S(1)}, s32[1024]{0:T(1024)S(1)}, u32[]{:S(2)}, u32[]{:S(2)}) %collective-permute-start.4) | collective-permute-done | bytes 4128 | tf_op jit(solution)/shard_map/ppermute | solution.py:19
  261.4 35.0 %collective-permute-start.5 = (s32[1024]{0:T(1024)S(1)}, s32[1024]{0:T(1024)S(1)}, u32[]{:S(2)}, u32[]{:S(2)}) collective-permute-start(s32[1024]{0:T(1024)S(1)} %get-tuple-element.329), channel_id=1, source_target_pairs={{0,1},{1,2},{2,3},{3,4},{4,5},{5,6},{6,7},{7,8},{8,9},{9,10},{10,1... | collective-permute-start | bytes 12296 | tf_op jit(solution)/shard_map/ppermute | solution.py:19
  380.8 286.8 %while.28 = (s32[]{:T(128)}, bf16[12,1024,64]{1,2,0:T(8,128)(2,1)S(1)}, f32[12,1024]{1,0:T(8,128)}, bf16[12,1024,64]{2,1,0:T(8,128)(2,1)}, bf16[12,5120,64]{2,1,...) while((s32[]{:T(128)}, ...), condition=%wide.region_3.4_spmd.clone, body=%wide.region_0.3_spmd.clone.sunk | while | flops 1420819456 | bytes 150063232 | solution.py:155
  702.4 15.3 convert_reduce_fusion
  761.6 793.3 %while.29 = (s32[]{:T(128)}, bf16[12,1024,64]{1,2,0:T(8,128)(2,1)S(1)}, f32[12,5120,64]{1,2,0:T(8,128)}, f32[12,5120,64]{1,2,0:T(8,128)}, bf16[12,1024,64]{2,1,0...) while((s32[]{:T(128)}, ...), condition=%wide.region_14.15_spmd.clone, body=%wide.region_12.14_spmd.clone.sunk | while | flops 3408264192 | bytes 228115728 | solution.py:208
  789.3 18.6 multiply_convert_fusion.3
  839.8 15.4 multiply_reduce_fusion.6
  855.2 20.3 multiply_convert_fusion.3
  909.4 15.2 multiply_reduce_fusion.6
  924.5 19.1 multiply_convert_fusion.3
  990.7 20.2 multiply_convert_fusion.3
  1059.4 19.0 multiply_convert_fusion.3
  1126.1 18.4 multiply_convert_fusion.3
  1191.3 18.4 multiply_convert_fusion.3
  1256.3 18.4 multiply_convert_fusion.3
  1321.4 18.4 multiply_convert_fusion.3
  1386.5 18.4 multiply_convert_fusion.3
  1451.6 18.4 multiply_convert_fusion.3
  1516.7 18.4 multiply_convert_fusion.3
  1554.9 18.5 fusion.71
  1588.2 332.0 %collective-permute-done.11 = f32[1024,1536]{0,1:T(8,128)S(1)} collective-permute-done((f32[1024,1536]{0,1:T(8,128)}, f32[1024,1536]{0,1:T(8,128)S(1)}, u32[]{:S(2)}, u32[]{:S(2)}) %collective-permute-start.11) | collective-permute-done | bytes 6291488 | tf_op jit(solution)/shard_map/ppermute | solution.py:19
  1953.8 103.1 %all-reduce.18 = (f32[768]{0:T(1024)S(1)}, f32[768]{0:T(1024)S(1)}, f32[768]{0:T(1024)S(1)}, f32[768]{0:T(1024)S(1)}, f32[768]{0:T(1024)S(1)}, /*index=5*/f32[30...) all-reduce(f32[768]{0:T(1024)S(1)} %get-tuple-element.242, ...), channel_id=3, replica_groups=mesh['fsdp'=32] {'fsdp'}, use_global_device_ids=true, to_apply=%region_17.18.clone | all-reduce | flops 9216 | bytes 73728
  2074.7 54.5 %reduce-scatter.13.cloned.1.call-done = f32[24,2304]{1,0:T(8,128)} async-done(((f32[768,2304]{1,0:T(8,128)}), f32[24,2304]{1,0:T(8,128)}) %reduce-scatter.13.cloned.1.call-update) | async-done | bytes 221200
  (489 shorter events, 1109.8 us)
Async XLA Ops:
  7.2 66.6 %all-gather.5.cloned.1.call-start = ((), (), s32[]{:S(2)}) async-start(), calls=%async_computation.4 | async-start | bytes 3649536 | tf_op jit(solution)/shard_map/all_gather | solution.py:90
  7.9 659.7 %all-gather.7.cloned.1.call-start = ((), (), s32[]{:S(2)}) async-start(), calls=%async_computation.5 | async-start | bytes 1216512 | tf_op jit(solution)/shard_map/all_gather | solution.py:93
  8.7 664.4 %all-gather.9.cloned.1.call-start = ((), (), s32[]{:S(2)}) async-start(), calls=%async_computation.6 | async-start | bytes 4866048 | tf_op jit(solution)/shard_map/all_gather | solution.py:97
  9.4 676.5 %all-gather.11.cloned.1.call-start = ((), (), s32[]{:S(2)}) async-start(), calls=%async_computation.7 | async-start | bytes 4866048 | tf_op jit(solution)/shard_map/all_gather | solution.py:99
  83.9 230.8 %collective-permute-start = (bf16[1024,1536]{1,0:T(8,128)(2,1)}, bf16[1024,1536]{1,0:T(8,128)(2,1)}, u32[]{:S(2)}, u32[]{:S(2)}) collective-permute-start(bf16[1024,1536]{1,0:T(8,128)(2,1)} %pad_maximum_fusion.2), channel_id=1, source_target_pairs={{0,2},{1,3},{2,4},{3,5},{4,6},{5,7},{6,8},{7,9},{8,10},{9,11},{10,... | collective-permute-start | bytes 9437192 | tf_op jit(solution)/shard_map/ppermute | solution.py:19
  89.0 227.8 %collective-permute-start.1 = (bf16[1024,1536]{1,0:T(8,128)(2,1)}, bf16[1024,1536]{1,0:T(8,128)(2,1)}, u32[]{:S(2)}, u32[]{:S(2)}) collective-permute-start(bf16[1024,1536]{1,0:T(8,128)(2,1)} %pad_maximum_fusion.2), channel_id=1, source_target_pairs={{0,1},{1,2},{2,3},{3,4},{4,5},{5,6},{6,7},{7,8},{8,9},{9,10},{10,1... | collective-permute-start | bytes 9437192 | tf_op jit(solution)/shard_map/ppermute | solution.py:19
  92.5 226.6 %collective-permute-start.2 = (bf16[1024,1536]{1,0:T(8,128)(2,1)}, bf16[1024,1536]{1,0:T(8,128)(2,1)}, u32[]{:S(2)}, u32[]{:S(2)}) collective-permute-start(bf16[1024,1536]{1,0:T(8,128)(2,1)} %pad_maximum_fusion.2), channel_id=1, source_target_pairs={{1,0},{2,1},{3,2},{4,3},{5,4},{6,5},{7,6},{8,7},{9,8},{10,9},{11,1... | collective-permute-start | bytes 9437192 | tf_op jit(solution)/shard_map/ppermute | solution.py:19
  93.8 227.5 %collective-permute-start.3 = (bf16[1024,1536]{1,0:T(8,128)(2,1)}, bf16[1024,1536]{1,0:T(8,128)(2,1)}, u32[]{:S(2)}, u32[]{:S(2)}) collective-permute-start(bf16[1024,1536]{1,0:T(8,128)(2,1)} %pad_maximum_fusion.2), channel_id=1, source_target_pairs={{2,0},{3,1},{4,2},{5,3},{6,4},{7,5},{8,6},{9,7},{10,8},{11,9},{12,... | collective-permute-start | bytes 9437192 | tf_op jit(solution)/shard_map/ppermute | solution.py:19
  95.1 166.2 %collective-permute-start.4 = (s32[1024]{0:T(1024)S(1)}, s32[1024]{0:T(1024)S(1)}, u32[]{:S(2)}, u32[]{:S(2)}) collective-permute-start(s32[1024]{0:T(1024)S(1)} %get-tuple-element.329), channel_id=1, source_target_pairs={{0,2},{1,3},{2,4},{3,5},{4,6},{5,7},{6,8},{7,9},{8,10},{9,11},{10,... | collective-permute-start | bytes 12296 | tf_op jit(solution)/shard_map/ppermute | solution.py:19
  99.7 1975.0 %reduce-scatter.7.cloned.1.call-start = ((), (), s32[]{:S(2)}) async-start(), calls=%async_computation.8 | async-start | bytes 2433024 | tf_op jit(solution)/shard_map/reduce_scatter | solution.py:231
  261.4 35.8 %collective-permute-start.5 = (s32[1024]{0:T(1024)S(1)}, s32[1024]{0:T(1024)S(1)}, u32[]{:S(2)}, u32[]{:S(2)}) collective-permute-start(s32[1024]{0:T(1024)S(1)} %get-tuple-element.329), channel_id=1, source_target_pairs={{0,1},{1,2},{2,3},{3,4},{4,5},{5,6},{6,7},{7,8},{8,9},{9,10},{10,1... | collective-permute-start | bytes 12296 | tf_op jit(solution)/shard_map/ppermute | solution.py:19
  297.2 4.0 collective-permute-start.6
  301.2 6.8 collective-permute-start.7
  380.8 288.0 %copy-start.22 = (f32[768]{0:T(1024)S(1)}, f32[768]{0:T(1024)}, u32[]{:S(2)}) copy-start(f32[768]{0:T(1024)} %convert_element_type.96) | copy-start | bytes 9220
  732.3 1342.3 %reduce-scatter.11.cloned.1.call-start = ((), (), s32[]{:S(2)}) async-start(), calls=%async_computation.10 | async-start | bytes 9732096 | tf_op jit(solution)/shard_map/reduce_scatter | solution.py:237
  742.3 1332.4 %reduce-scatter.9.cloned.1.call-start = ((), (), s32[]{:S(2)}) async-start(), calls=%async_computation.9 | async-start | bytes 9732096 | tf_op jit(solution)/shard_map/reduce_scatter | solution.py:235
  761.3 1367.9 %reduce-scatter.13.cloned.1.call-start = ((), (), s32[]{:S(2)}) async-start(), calls=%async_computation.11 | async-start | bytes 7299072
  855.1 29.0 %slice-start.1 = ((s8[20971520]{0:T(1024)(128)(4,1)}), s8[4194304]{0:T(1024)(128)(4,1)S(1)}, s32[]{:S(2)}) async-start(s8[20971520]{0:T(1024)(128)(4,1)} %bitcast.147), calls=%async_computation.13 | async-start | bytes 8388608 | tf_op jit(solution)/shard_map/while
  855.1 29.0 %slice-start.2 = ((s8[20971520]{0:T(1024)(128)(4,1)}), s8[4194304]{0:T(1024)(128)(4,1)S(1)}, s32[]{:S(2)}) async-start(s8[20971520]{0:T(1024)(128)(4,1)} %bitcast.147), calls=%async_computation.14 | async-start | bytes 8388608 | tf_op jit(solution)/shard_map/while
  1573.3 14.9 collective-permute-start.10
  1578.7 341.6 %collective-permute-start.11 = (f32[1024,1536]{0,1:T(8,128)}, f32[1024,1536]{0,1:T(8,128)S(1)}, u32[]{:S(2)}, u32[]{:S(2)}) collective-permute-start(f32[1024,1536]{0,1:T(8,128)} %get-tuple-element.319), channel_id=1, source_target_pairs={{0,2},{1,3},{2,4},{3,5},{4,6},{5,7},{6,8},{7,9},{8,10},{9,11},{10,... | collective-permute-start | bytes 18874376 | tf_op jit(solution)/shard_map/ppermute | solution.py:19
  1582.2 338.0 %collective-permute-start.8 = (f32[1024,1536]{0,1:T(8,128)}, f32[1024,1536]{0,1:T(8,128)S(1)}, u32[]{:S(2)}, u32[]{:S(2)}) collective-permute-start(f32[1024,1536]{0,1:T(8,128)} %get-tuple-element.317), channel_id=1, source_target_pairs={{2,0},{3,1},{4,2},{5,3},{6,4},{7,5},{8,6},{9,7},{10,8},{11,9},{12,... | collective-permute-start | bytes 18874376 | tf_op jit(solution)/shard_map/ppermute | solution.py:19
  1583.5 339.3 %collective-permute-start.9 = (f32[1024,1536]{0,1:T(8,128)}, f32[1024,1536]{0,1:T(8,128)}, u32[]{:S(2)}, u32[]{:S(2)}) collective-permute-start(f32[1024,1536]{0,1:T(8,128)} %get-tuple-element.318), channel_id=1, source_target_pairs={{1,0},{2,1},{3,2},{4,3},{5,4},{6,5},{7,6},{8,7},{9,8},{10,9},{11,1... | collective-permute-start | bytes 18874376 | tf_op jit(solution)/shard_map/ppermute | solution.py:19
  1953.1 108.5 %copy-start.12 = (f32[1024]{0:T(1024)S(1)}, f32[1024]{0:T(1024)}, u32[]{:S(2)}) copy-start(f32[1024]{0:T(1024)} %copy-done.11) | copy-start | bytes 12292
  (99 other events, 1596.5 us)
Sparse Core Ops, SparseCore 0:
  10.9 62.8 all-gather.4
  76.7 148.9 all-gather.6
  228.6 115.9 all-gather.8
  347.3 61.9 all-gather.10
  732.5 102.8 reduce-scatter.6
  841.6 135.2 reduce-scatter.10
  983.4 135.1 reduce-scatter.8
  1947.9 181.3 reduce-scatter.12
where the time goes:
time: 2150 us; the launch traced here: 2140 us
  matrix products  839 us (39%)
  waiting for transfers between devices  568 us (26%)
  other arithmetic  342 us (16%)
  local copies, waits for them, and re-layouts  160 us (7%)
  blocking collectives  146 us (7%)
  starting transfers between devices  65.2 us (3%)
    ppermute x12, waiting for transfers between devices, from_behind(): return lax.ppermute(block, axis, route)  496 us
    dot_general x24, matrix products, head_scores(): jnp.einsum('qd,kd->qk', q_head, k_head, preferred_element_type=jnp.float32)  238 us
    convert_element_type x12, other arithmetic, head_backward(): d_scores = (probs * (d_probs - inner)).astype(jnp.bfloat16)  226 us
    unnamed x2, blocking collectives  146 us
    dot_general x12, matrix products, probs_inner(): jnp.einsum('qd,kd->qk', d_ctx, v_head, preferred_element_type=jnp.float32)  136 us
    dot_general x12, matrix products, head_forward(): context = jnp.dot(probs_low, v_head, preferred_element_type=jnp.float32)  126 us
    dot_general x12, matrix products, head_backward(): jnp.einsum('qk,qd->kd', d_scores, q_head, preferred_element_type=jnp.floa...  98.2 us
    dot_general x12, matrix products, head_backward(): jnp.dot(d_scores, k_head, preferred_element_type=jnp.float32) * score_scale  92.2 us
  transfers between devices with their start and end apart: 20, of which 8 were waited for; matrix products, arithmetic and copies ran while one was open for 60% of the time, Pallas kernels for 0%

commit v1 on v0

v1 whole, which is shorter than its diff:
```python
import functools

import jax
import jax.numpy as jnp
from jax import lax
from jax.experimental import pallas as pl
from jax.experimental.pallas import tpu as pltpu
from jax.sharding import PartitionSpec as P

D = 768
HEADS = 12
HEAD_DIM = 64
LEN_MAX = 2048
GROUP = 4
OWN_HEADS = HEADS // GROUP
Q_ROWS = OWN_HEADS * HEAD_DIM
KV_ROWS = 2 * Q_ROWS
MIX_ROWS = Q_ROWS + KV_ROWS
BQ = 256
BK = 256
NEG = -1e30

bf16 = jnp.bfloat16
f32 = jnp.float32
eps_norm = 1e-12
score_scale = 0.125

NN = (((1,), (0,)), ((), ()))
NT = (((1,), (1,)), ((), ()))


def mm(a, b, dims=NN):
    return lax.dot_general(a, b, dims, preferred_element_type=f32)


def norm_rows(hidden, gain_row, shift_row):
    centre = hidden - jnp.mean(hidden, axis=-1, keepdims=True)
    spread = jnp.mean(centre * centre, axis=-1, keepdims=True)
    return centre * lax.rsqrt(spread + eps_norm) * gain_row + shift_row


def gelu_exact(pre_act):
    return 0.5 * pre_act * (1.0 + jax.scipy.special.erf(pre_act * 0.7071067811865476))


def head_rows(block, h, upper):
    zero = jnp.zeros_like(block[:HEAD_DIM])
    rows = block[h * HEAD_DIM : (h + 1) * HEAD_DIM]
    return jnp.concatenate([zero, rows] if upper else [rows, zero], axis=0)


def attend_kernel(
    span, qtag_ref, ktag_ref, qt_ref, kv_ref, kvt_ref, ot_ref, lse_ref, m_sc, l_sc, acc_sc
):
    i = pl.program_id(0)
    m_sc[...] = jnp.full_like(m_sc, NEG)
    l_sc[...] = jnp.zeros_like(l_sc)
    acc_sc[...] = jnp.zeros_like(acc_sc)
    qtag = qtag_ref[...]
    qt = qt_ref[...]
    q_pad = [head_rows(qt, h, False) for h in range(OWN_HEADS)]

    def step(kb, carry):
        rows = pl.ds(pl.multiple_of(kb * BK, BK), BK)
        seen = ktag_ref[rows, :] == qtag
        for h in range(OWN_HEADS):
            s = mm(kv_ref[rows, 128 * h : 128 * (h + 1)], q_pad[h])
            s = jnp.where(seen, s, NEG)
            m_old = m_sc[h : h + 1, :]
            m_new = jnp.maximum(m_old, jnp.max(s, axis=0, keepdims=True))
            p = jnp.exp(s - m_new)
            fade = jnp.exp(m_old - m_new)
            l_sc[h : h + 1, :] = fade * l_sc[h : h + 1, :] + jnp.sum(p, axis=0, keepdims=True)
            m_sc[h : h + 1, :] = m_new
            own = slice(HEAD_DIM * h, HEAD_DIM * (h + 1))
            v_t = kvt_ref[128 * h + HEAD_DIM : 128 * (h + 1), rows]
            acc_sc[own, :] = acc_sc[own, :] * fade + mm(v_t, p.astype(bf16))
        return carry

    lax.fori_loop(span[i, 0], span[i, 1], step, 0)
    for h in range(OWN_HEADS):
        own = slice(HEAD_DIM * h, HEAD_DIM * (h + 1))
        total = l_sc[h : h + 1, :]
        ot_ref[own, :] = (acc_sc[own, :] / total).astype(bf16)
        lse_ref[h : h + 1, :] = m_sc[h : h + 1, :] + jnp.log(total)
    lse_ref[OWN_HEADS:, :] = jnp.zeros_like(lse_ref[OWN_HEADS:, :])


def attend(span, qtag, ktag, qt, kv, kvt):
    own = qt.shape[1]
    window = kv.shape[0]
    whole = lambda shape: pl.BlockSpec(shape, lambda i, s: (0, 0), pipeline_mode=pl.Buffered(1))
    cols = lambda rows: pl.BlockSpec((rows, BQ), lambda i, s: (0, i))
    return pl.pallas_call(
        attend_kernel,
        grid_spec=pltpu.PrefetchScalarGridSpec(
            num_scalar_prefetch=1,
            grid=(own // BQ,),
            in_specs=[
                cols(1),
                whole((window, 1)),
                cols(Q_ROWS),
                whole((window, KV_ROWS)),
                whole((KV_ROWS, window)),
            ],
            out_specs=[cols(Q_ROWS), cols(8)],
            scratch_shapes=[
                pltpu.VMEM((8, BQ), f32),
                pltpu.VMEM((8, BQ), f32),
                pltpu.VMEM((Q_ROWS, BQ), f32),
            ],
        ),
        out_shape=[
            jax.ShapeDtypeStruct((Q_ROWS, own), bf16),
            jax.ShapeDtypeStruct((8, own), f32),
        ],
        compiler_params=pltpu.CompilerParams(vmem_limit_bytes=60 << 20),
        cost_estimate=pl.CostEstimate(
            flops=4 * own * 2048 * Q_ROWS, bytes_accessed=20 << 20, transcendentals=own * 6144
        ),
        name="attend",
    )(span, qtag, ktag, qt, kv, kvt)


def grad_kernel(
    parts, final, span, qtag_ref, ktag_ref, qt_ref, dot_ref, ot_ref, lse_ref, kv_ref, kvt_ref, *rest
):
    if final:
        dq_in, dq_ref, *rest = rest
    else:
        dq_in, (dq_ref, *rest) = None, rest
    outs, (dq_sc, dkv_sc) = rest[: len(parts)], rest[len(parts) :]
    i = pl.program_id(0)

    @pl.when(i == 0)
    def _():
        dkv_sc[...] = jnp.zeros_like(dkv_sc)

    if final:
        dq_sc[...] = dq_in[...]
    else:
        dq_sc[...] = jnp.zeros_like(dq_sc)
    qtag = qtag_ref[...]
    qt, d_out, out = qt_ref[...], dot_ref[...], ot_ref[...]
    q_pad = [head_rows(qt, h, False) for h in range(OWN_HEADS)]
    d_pad = [head_rows(d_out, h, True) for h in range(OWN_HEADS)]
    both = [jnp.concatenate([q_pad[h], d_pad[h]], axis=1) for h in range(OWN_HEADS)]
    product = d_out.astype(f32) * out.astype(f32)
    inner = [
        jnp.sum(product[HEAD_DIM * h : HEAD_DIM * (h + 1)], axis=0, keepdims=True)
        for h in range(OWN_HEADS)
    ]
    log_row = [lse_ref[h : h + 1, :] for h in range(OWN_HEADS)]

    def step(shift, kb, carry):
        rows = pl.ds(pl.multiple_of(kb * BK, BK), BK)
        place = pl.ds(pl.multiple_of((kb - shift) * BK, BK), BK)
        seen = ktag_ref[rows, :] == qtag
        for h in range(OWN_HEADS):
            kv_h = kv_ref[rows, 128 * h : 128 * (h + 1)]
            s = mm(kv_h, q_pad[h])
            p = jnp.where(seen, jnp.exp(s - log_row[h]), 0.0)
            d_p = mm(kv_h, d_pad[h])
            d_s = (p * (d_p - inner[h])).astype(bf16)
            pair = jnp.concatenate([d_s, p.astype(bf16)], axis=1)
            span_rows = slice(128 * h, 128 * (h + 1))
            dkv_sc[span_rows, place] += mm(both[h], pair, NT)
            own = slice(HEAD_DIM * h, HEAD_DIM * (h + 1))
            dq_sc[own, :] += mm(kvt_ref[128 * h : 128 * h + HEAD_DIM, rows], d_s)
        return carry

    base = 0
    for n, (first, last) in enumerate(parts):
        low = jnp.maximum(span[i, 0], first)
        high = jnp.minimum(span[i, 1], last)
        lax.fori_loop(low, high, functools.partial(step, first - base), 0)
        base += last - first
    if final:
        dq_ref[...] = (dq_sc[...] * score_scale).astype(bf16)
    else:
        dq_ref[...] = dq_sc[...]

    @pl.when(i == pl.num_programs(0) - 1)
    def _():
        base = 0
        for (first, last), ref in zip(parts, outs):
            width = (last - first) * BK
            ref[...] = dkv_sc[:, base : base + width].astype(ref.dtype)
            base += width


def attend_grad(parts, final, span, qtag, ktag, qt, d_out, out, lse, kv, kvt, dq_in=None):
    own = qt.shape[1]
    window = kv.shape[0]
    whole = lambda shape: pl.BlockSpec(shape, lambda i, s: (0, 0), pipeline_mode=pl.Buffered(1))
    cols = lambda rows: pl.BlockSpec((rows, BQ), lambda i, s: (0, i))
    widths = [(last - first) * BK for first, last in parts]
    dtype = f32 if final else bf16
    args = [span, qtag, ktag, qt, d_out, out, lse, kv, kvt] + ([dq_in] if final else [])
    return pl.pallas_call(
        functools.partial(grad_kernel, parts, final),
        grid_spec=pltpu.PrefetchScalarGridSpec(
            num_scalar_prefetch=1,
            grid=(own // BQ,),
            in_specs=[
                cols(1),
                whole((window, 1)),
                cols(Q_ROWS),
                cols(Q_ROWS),
                cols(Q_ROWS),
                cols(8),
                whole((window, KV_ROWS)),
                whole((KV_ROWS, window)),
            ]
            + ([cols(Q_ROWS)] if final else []),
            out_specs=[cols(Q_ROWS)] + [whole((KV_ROWS, w)) for w in widths],
            scratch_shapes=[
                pltpu.VMEM((Q_ROWS, BQ), f32),
                pltpu.VMEM((KV_ROWS, sum(widths)), f32),
            ],
        ),
        out_shape=[jax.ShapeDtypeStruct((Q_ROWS, own), bf16 if final else f32)]
        + [jax.ShapeDtypeStruct((KV_ROWS, w), dtype) for w in widths],
        compiler_params=pltpu.CompilerParams(vmem_limit_bytes=60 << 20),
        cost_estimate=pl.CostEstimate(
            flops=(10 if final else 2) * own * 1536 * Q_ROWS,
            bytes_accessed=20 << 20,
            transcendentals=own * 4096,
        ),
        name="grad_own" if final else "grad_far",
    )(*args)


def body(
    n_dev,
    tokens,
    segment_ids,
    pad_mask,
    w_qkv,
    bias_query,
    bias_value,
    w_out,
    bias_out,
    gain_one,
    shift_one,
    w_up,
    bias_up,
    w_down,
    bias_down,
    gain_two,
    shift_two,
    cotangent,
):
    row_count = tokens.shape[0]
    rows_w = w_qkv.shape[0]
    own = GROUP * row_count
    window = own + 2 * LEN_MAX
    me = lax.axis_index("fsdp")
    place = me % GROUP
    group_id = me // GROUP
    n_group = n_dev // GROUP
    groups = [[GROUP * g + j for j in range(GROUP)] for g in range(n_group)]

    wq = w_qkv[:, :D].reshape(rows_w, GROUP, Q_ROWS)
    wk = w_qkv[:, D : 2 * D].reshape(rows_w, GROUP, OWN_HEADS, 1, HEAD_DIM)
    wv = w_qkv[:, 2 * D :].reshape(rows_w, GROUP, OWN_HEADS, 1, HEAD_DIM)
    wkv = jnp.concatenate([wk, wv], axis=3).reshape(rows_w, GROUP, KV_ROWS)
    w_cut = jnp.concatenate([wq, wkv], axis=2).transpose(1, 0, 2)
    w_send = jnp.tile(w_cut, (n_group, 1, 1))
    w_mix = lax.all_to_all(w_send, "fsdp", 0, 0, tiled=True).reshape(D, MIX_ROWS)
    small = jnp.concatenate(
        [bias_query, bias_value, bias_out, gain_one, shift_one, bias_down, gain_two, shift_two, bias_up]
    )
    small_all = lax.all_gather(small, "fsdp", axis=0, tiled=False)
    rows8 = small_all[:, : 8 * rows_w].reshape(n_dev, 8, rows_w).transpose(1, 0, 2).reshape(8, D)
    rows8 = rows8.astype(f32)
    bu_full = small_all[:, 8 * rows_w :].reshape(-1).astype(f32)
    bq_full, bv_full, bo_full, g1_full, s1_full, bd_full, g2_full, s2_full = [
        rows8[j] for j in range(8)
    ]
    big = jnp.concatenate([w_out, w_up, w_down.reshape(rows_w, -1)], axis=1)
    big_all = lax.all_gather(big, "fsdp", axis=0, tiled=True)
    ff = w_up.shape[1]
    wo_full = big_all[:, :D]
    wu_full = big_all[:, D : D + ff]
    wd_full = big_all[:, D + ff :].reshape(ff, D)

    code = segment_ids * 2 + pad_mask
    x_own = lax.all_gather(tokens, "fsdp", axis=0, tiled=True, axis_index_groups=groups)
    code_own = lax.all_gather(code, "fsdp", axis=0, tiled=True, axis_index_groups=groups)
    up = [(i, i + GROUP) for i in range(n_dev - GROUP)]
    down = [(i + GROUP, i) for i in range(n_dev - GROUP)]
    x_left, c_left = lax.ppermute((x_own[own - LEN_MAX :], code_own[own - LEN_MAX :]), "fsdp", up)
    x_right, c_right = lax.ppermute((x_own[:LEN_MAX], code_own[:LEN_MAX]), "fsdp", down)
    x_win = jnp.concatenate([x_left, x_own, x_right], axis=0)
    c_left = jnp.where(group_id == 0, -2, c_left)
    c_right = jnp.where(group_id == n_group - 1, 2 * n_dev * row_count, c_right)
    code_win = jnp.concatenate([c_left, code_own, c_right])
    seg_win = code_win >> 1
    ktag = jnp.where((code_win & 1) == 1, seg_win + 1, 0).reshape(window, 1)
    seg_own = code_own >> 1
    qtag = (seg_own + 1).reshape(1, own)
    first_seg = seg_own[::BQ]
    last_seg = seg_own[BQ - 1 :: BQ]
    low = jnp.sum((seg_win[None, :] < first_seg[:, None]).astype(jnp.int32), axis=1)
    high = jnp.sum((seg_win[None, :] <= last_seg[:, None]).astype(jnp.int32), axis=1)
    span = jnp.stack([low // BK, (high + BK - 1) // BK], axis=1)

    bq = lax.dynamic_slice(bq_full, (place * Q_ROWS,), (Q_ROWS,))
    bv = lax.dynamic_slice(bv_full, (place * Q_ROWS,), (Q_ROWS,)).reshape(OWN_HEADS, 1, HEAD_DIM)
    bkv = jnp.concatenate([jnp.zeros_like(bv), bv], axis=1).reshape(KV_ROWS)
    w_q, w_kv = w_mix[:, :Q_ROWS], w_mix[:, Q_ROWS:]
    qt = jnp.einsum("dc,td->ct", w_q, x_own, preferred_element_type=f32) + bq[:, None]
    qt = qt.astype(bf16) * jnp.asarray(score_scale, bf16)
    kv = (jnp.dot(x_win, w_kv, preferred_element_type=f32) + bkv).astype(bf16)
    kvt = jnp.einsum("dc,td->ct", w_kv, x_win, preferred_element_type=f32) + bkv[:, None]
    kvt = kvt.astype(bf16)

    ot, lse = attend(span, qtag, ktag, qt, kv, kvt)
    ctx_t = lax.all_to_all(
        ot.reshape(Q_ROWS, GROUP, row_count), "fsdp", 1, 0, axis_index_groups=groups, tiled=True
    ).reshape(D, row_count)

    tokens_f = tokens.astype(f32)
    branch = jnp.einsum("ir,io->ro", ctx_t, wo_full, preferred_element_type=f32) + bo_full
    first, norm_one_back = jax.vjp(norm_rows, tokens_f + branch, g1_full, s1_full)
    up_in = first.astype(bf16)
    pre_act = jnp.dot(up_in, wu_full, preferred_element_type=f32) + bu_full
    gelu_val, gelu_back = jax.vjp(gelu_exact, pre_act)
    hidden = gelu_val.astype(bf16)
    ffn = jnp.dot(hidden, wd_full, preferred_element_type=f32) + bd_full
    result, norm_two_back = jax.vjp(norm_rows, first + ffn, g2_full, s2_full)
    layer_out = result.astype(bf16)
    d_second, d_gain_two, d_shift_two = norm_two_back(cotangent.astype(f32))
    d_ffn = d_second.astype(bf16)
    d_bias_down = jnp.sum(d_ffn.astype(f32), axis=0)
    d_w_down = jnp.einsum("rf,rd->fd", hidden, d_ffn, preferred_element_type=f32)
    d_hidden = jnp.einsum("rd,fd->rf", d_ffn, wd_full, preferred_element_type=f32)
    d_pre = gelu_back(d_hidden)[0].astype(bf16)
    d_bias_up = jnp.sum(d_pre.astype(f32), axis=0)
    d_w_up = jnp.einsum("rd,rf->df", up_in, d_pre, preferred_element_type=f32)
    d_first = d_second + jnp.einsum("rf,df->rd", d_pre, wu_full, preferred_element_type=f32)
    d_mid, d_gain_one, d_shift_one = norm_one_back(d_first)
    d_branch = d_mid.astype(bf16)
    d_bias_out = jnp.sum(d_branch.astype(f32), axis=0)
    d_w_out = jnp.einsum("ir,ro->io", ctx_t, d_branch, preferred_element_type=f32)
    dctx_t = jnp.einsum("ro,io->ir", d_branch, wo_full, preferred_element_type=f32).astype(bf16)
    big_grad = jnp.concatenate(
        [d_w_out.astype(bf16), d_w_up.astype(bf16), d_w_down.astype(bf16).reshape(D, ff)], axis=1
    )
    big_owned = lax.psum_scatter(big_grad, "fsdp", scatter_dimension=0, tiled=True).astype(f32)

    d_out = lax.all_to_all(
        dctx_t.reshape(GROUP, Q_ROWS, row_count), "fsdp", 0, 2, axis_index_groups=groups, tiled=True
    ).reshape(Q_ROWS, own)
    edge, inside = LEN_MAX // BK, own // BK
    far_parts = ((0, edge), (edge + inside, 2 * edge + inside))
    own_parts = ((edge, edge + inside),)
    dq_far, dkv_left, dkv_right = attend_grad(
        far_parts, False, span, qtag, ktag, qt, d_out, ot, lse, kv, kvt
    )
    from_right = lax.ppermute(dkv_left, "fsdp", down)
    from_left = lax.ppermute(dkv_right, "fsdp", up)
    dq_t, dkv_own = attend_grad(
        own_parts, True, span, qtag, ktag, qt, d_out, ot, lse, kv, kvt, dq_far
    )
    dkv = jnp.concatenate(
        [
            dkv_own[:, :LEN_MAX] + from_left.astype(f32),
            dkv_own[:, LEN_MAX : own - LEN_MAX],
            dkv_own[:, own - LEN_MAX :] + from_right.astype(f32),
        ],
        axis=1,
    ).astype(bf16)
    dmix_t = jnp.concatenate([dq_t, dkv], axis=0)
    dmix_sum = jnp.sum(dmix_t.astype(f32), axis=1)
    d_w_mix = jnp.einsum("td,ct->dc", x_own, dmix_t, preferred_element_type=f32)
    d_x = jnp.einsum("ct,dc->td", dmix_t, w_mix, preferred_element_type=f32)
    grad_tokens = d_mid + lax.psum_scatter(
        d_x, "fsdp", scatter_dimension=0, tiled=True, axis_index_groups=groups
    )
    got = lax.all_to_all(
        d_w_mix.reshape(n_dev, rows_w, MIX_ROWS), "fsdp", 0, 0, tiled=True
    ).reshape(n_group, GROUP, rows_w, MIX_ROWS)
    got = jnp.sum(got, axis=0).transpose(1, 0, 2)
    g_q = got[:, :, :Q_ROWS].reshape(rows_w, D)
    g_kv = got[:, :, Q_ROWS:].reshape(rows_w, GROUP, OWN_HEADS, 2, HEAD_DIM)
    g_k = g_kv[:, :, :, 0].reshape(rows_w, D)
    g_v = g_kv[:, :, :, 1].reshape(rows_w, D)
    grad_w_qkv = jnp.concatenate([g_q, g_k, g_v], axis=1)

    pad_vec = lambda v: lax.dynamic_update_slice(jnp.zeros((D,), f32), v, (place * Q_ROWS,))
    d_bq = pad_vec(dmix_sum[:Q_ROWS])
    d_bv = pad_vec(dmix_sum[Q_ROWS:].reshape(OWN_HEADS, 2, HEAD_DIM)[:, 1].reshape(Q_ROWS))
    vecs = jnp.stack(
        [d_bq, d_bv, d_bias_out, d_gain_one, d_shift_one, d_bias_down, d_gain_two, d_shift_two]
    )
    vec_send = jnp.concatenate(
        [
            vecs.reshape(8, n_dev, rows_w).transpose(1, 0, 2).reshape(n_dev, 8 * rows_w),
            d_bias_up.reshape(n_dev, 4 * rows_w),
        ],
        axis=1,
    )
    vec = lax.psum_scatter(vec_send, "fsdp", scatter_dimension=0, tiled=True)[0]
    own_vec = [vec[j * rows_w : (j + 1) * rows_w] for j in range(8)]
    return (
        layer_out,
        grad_tokens,
        grad_w_qkv,
        own_vec[0],
        own_vec[1],
        big_owned[:, :D],
        own_vec[2],
        own_vec[3],
        own_vec[4],
        big_owned[:, D : D + ff],
        vec[8 * rows_w :],
        big_owned[:, D + ff :].reshape(4 * rows_w, D),
        own_vec[5],
        own_vec[6],
        own_vec[7],
    )


def solution(mesh):
    rows, flat = P("fsdp", None), P("fsdp")
    return jax.shard_map(
        functools.partial(body, mesh.shape["fsdp"]),
        mesh=mesh,
        in_specs=(
            rows, flat, flat, rows, flat, flat, rows, flat, flat, flat, rows, flat, rows, flat,
            flat, flat, rows,
        ),
        out_specs=(
            rows, rows, rows, flat, flat, rows, flat, flat, flat, rows, flat, rows, flat, flat,
            flat,
        ),
        check_vma=False,
    )
```

time: 2150 us -> 923 us (0.43)
  matrix products: 839 us -> 118 us
  waiting for transfers between devices: 568 us -> 173 us
  other arithmetic: 342 us -> 41 us
  Pallas kernels: 0 us -> 276 us
  local copies, waits for them, and re-layouts: 160 us -> 83.8 us
    dot_general x96 -> x14, matrix products: 839 us -> 118 us  [the longest x1 14.3 us: body(): jnp.einsum('rd,fd->rf', d_ffn, wd_full, preferred_element_type=f32)]
    ppermute x12 -> x6, waiting for transfers between devices: 496 us -> 142 us  [the longest x2 142 us: body(): lax.ppermute((x_own[own - LEN_MAX:], code_own[own - LEN_MAX:]), 'fsdp', up)]
    pallas_call x0 -> x3, Pallas kernels: none -> 276 us  [the longest x2 159 us: attend_grad(): pl.pallas_call(functools.partial(grad_kernel, parts, final), grid_spec=pl...]
    convert_element_type x22 -> x2, other arithmetic: 233 us -> 0.08 us  [the longest x1 0.07 us: body(): bu_full = small_all[:, 8 * rows_w:].reshape(-1).astype(f32)]
    reduce_sum x15 -> x5, other arithmetic: 73.4 us -> 8.22 us  [the longest x1 3.06 us: body(): dmix_sum = jnp.sum(dmix_t.astype(f32), axis=1)]
    unnamed x104 -> x62, local copies, waits for them, and re-layouts: 79.8 us -> 20.1 us
    unnamed x9 -> x4, waiting for transfers between devices: 56.7 us -> 0.73 us
    unnamed x2, blocking collectives: 146 us -> 102 us
  transfers between devices with their start and end apart: 20 -> 13, of which waited for: 8 -> 3; matrix products, arithmetic and copies ran while one was open for 60% -> 14% of each run, Pallas kernels for 0% -> 30%
where the time goes in v1:
time: 923 us; the launch traced here: 925 us
  Pallas kernels  276 us (30%)
  waiting for transfers between devices  173 us (19%)
  blocking collectives  139 us (15%)
  matrix products  118 us (13%)
  local copies, waits for them, and re-layouts  83.8 us (9%)
  starting transfers between devices  79.4 us (9%)
  other arithmetic  41 us (4%)
  between operations  15.1 us (2%)
    pallas_call x2, Pallas kernels, attend_grad(): pl.pallas_call(functools.partial(grad_kernel, parts, final), grid_spec=pl...  159 us
    ppermute x2, waiting for transfers between devices, body(): lax.ppermute((x_own[own - LEN_MAX:], code_own[own - LEN_MAX:]), 'fsdp', up)  142 us
    pallas_call x1, Pallas kernels, attend(): pl.pallas_call(attend_kernel, grid_spec=pltpu.PrefetchScalarGridSpec(num_...  116 us
    unnamed x2, blocking collectives  102 us
    ppermute x1, starting transfers between devices, body(): from_left = lax.ppermute(dkv_right, 'fsdp', up)  33.8 us
    all_to_all x1, blocking collectives, body(): lax.all_to_all(dctx_t.reshape(GROUP, Q_ROWS, row_count), 'fsdp', 0, 2, ax...  22.7 us
    all_to_all x1, starting transfers between devices, body(): lax.all_to_all(d_w_mix.reshape(n_dev, rows_w, MIX_ROWS), 'fsdp', 0, 0, ti...  21.8 us
    unnamed x62, local copies, waits for them, and re-layouts  20.1 us
  transfers between devices with their start and end apart: 13, of which 3 were waited for; matrix products, arithmetic and copies ran while one was open for 14% of the time, Pallas kernels for 30%

profile of v1, /device:TPU:0, one launch (start us, length us, event | category | flops | bytes accessed | tf_op | source)
XLA Modules:
  0.0 925.3 jit_solution(4606393749227094853)
XLA Ops:
  13.7 7.4 all-to-all-start
  21.2 14.5 %all_gather.15 = s32[4096]{0:T(1024)S(1)} all-gather(s32[1024]{0:T(1024)S(1)} %multiply_add_fusion.3), channel_id=1, replica_groups={{0,1,2,3},{4,5,6,7},{8,9,10,11},{12,13,14,15},{16,17,18,19},{20,21,22,2..., dimensions={0}, use_global_device_ids=true | all-gather | bytes 20480 | tf_op jit(solution)/shard_map/all_gather | solution.py:290
  40.5 41.8 %all-reduce.1 = bf16[9216]{0:T(1024)(128)(2,1)S(1)} all-reduce(bf16[9216]{0:T(1024)(128)(2,1)S(1)} %dynamic-update-slice), channel_id=2, replica_groups=mesh['fsdp'=32] {'fsdp'}, use_global_device_ids=true, to_apply=%add.1 | all-reduce | flops 9216 | bytes 36864
  115.4 141.8 %collective-permute-done.2 = bf16[2048,768]{1,0:T(8,128)(2,1)S(1)} collective-permute-done((bf16[2048,768]{1,0:T(8,128)(2,1)}, bf16[2048,768]{1,0:T(8,128)(2,1)S(1)}, u32[]{:S(2)}, u32[]{:S(2)}) %collective-permute-start.2) | collective-permute-done | bytes 3145760 | tf_op jit(solution)/shard_map/ppermute | solution.py:293
  265.8 12.1 %add_convert_fusion.1.kvt_ref = bf16[384,8192]{1,0:T(8,128)(2,1)} fusion(bf16[8192,768]{1,0:T(8,128)(2,1)} %constant_dynamic-update-slice_fusion, f32[384]{0:T(512)S(1)} %add.192, bf16[768,576]{1,0:T(8,128)(2,1)} %bitcast.8), kind=kOutput, calls=%fused_computation.4 | convolution fusion | flops 4838129664 | bytes 19465728 | tf_op jit(solution)/shard_map/dc,td->ct/dot_general | solution.py:316
  277.9 10.0 %add_convert_fusion.2.kv_ref = bf16[8192,384]{1,0:T(8,128)(2,1)} fusion(bf16[8192,768]{1,0:T(8,128)(2,1)S(1)} %copy-done.9, f32[384]{0:T(512)S(1)} %add.192, bf16[768,576]{1,0:T(8,128)(2,1)} %bitcast.8), kind=kOutput, calls=%fused_computation.5 | convolution fusion | flops 4838129664 | bytes 19465728 | tf_op jit(solution)/shard_map/dot_general | solution.py:315
  287.9 116.2 %attend.1 = (bf16[192,4096]{1,0:T(8,128)(2,1)}, f32[8,4096]{1,0:T(8,128)}) custom-call(s32[16,2]{1,0:T(8,128)} %copy.136.span, s32[1,4096]{1,0:T(1,128)} %bitcast.108, s32[8192,1]{1,0:T(8,128)} %fusion.2.ktag_ref, bf16[192,4096]{1,0:T(8,128)(2,1)} %fusion.1.qt_ref, bf16[8192,384]{1,0:T(8,128)(2,1)} %add_convert_fusion.2.kv_ref, ...), custom_call_target="tpu_custom_call" | custom-call | flops 6442450944 | bytes 20971520 | tf_op jit(solution)/shard_map/attend/pallas_call | solution.py:94
  414.9 16.7 %all-to-all-done.1 = bf16[192,4,1024]{2,0,1:T(8,128)(2,1)} async-done(((bf16[192,4,1024]{2,0,1:T(8,128)(2,1)}), bf16[192,4,1024]{2,0,1:T(8,128)(2,1)}, u32[]{:S(2)}, u32[]{:S(2)}) %all-to-all-start.1) | async-done | bytes 1572896 | tf_op jit(solution)/shard_map/all_to_all | solution.py:320
  442.3 8.5 reshape.453
  450.8 13.2 %multiply_convert_fusion = (bf16[1024,3072]{1,0:T(8,128)(2,1)S(1)}, f32[1024,3072]{1,0:T(8,128)}) fusion(f32[3072]{0:T(1024)S(1)} %reshape.465, bf16[768,6912]{1,0:T(8,128)(2,1)} %all-gather.6.cloned.1.call-done, f32[1024,768]{0,1:T(8,128)} %copy-done, f32[768]{0:T(1024)S(1)} %add.202, f32[768]{0:T(1024)S(1)} %mul.166, f32[1024]{0:T(1024)S(1)} %fusion.19, ...), kind=kOutput, calls=%fused_computation.2 | convolution fusion | flops 4854644736 | bytes 26765312 | tf_op jit(solution)/shard_map/dot_general | solution.py:328
  482.3 14.3 %convert_reduce_fusion = (f32[3072]{0:T(1024)S(1)}, bf16[1024,3072]{1,0:T(8,128)(2,1)S(1)}) fusion(bf16[1024,768]{0,1:T(8,128)(2,1)S(1)} %get-tuple-element.123, bf16[3072,768]{1,0:T(8,128)(2,1)S(1)} %copy-done.5, f32[1024,3072]{1,0:T(8,128)} %get-tuple-element.159, f32[3072]{0:T(1024)S(1)} %reshape.465), kind=kOutput, calls=%fused_computation | convolution fusion | flops 4882166784 | bytes 25190400 | tf_op jit(solution)/shard_map/rd,fd->rf/dot_general | solution.py:338
  496.6 7.1 convolution_convert_fusion.1
  503.7 9.0 multiply_reduce_fusion
  521.3 8.5 reshape.463
  529.8 9.1 pad_maximum_fusion
  542.1 22.7 %all_to_all.40 = bf16[4,192,1024]{2,1,0:T(8,128)(2,1)S(1)} all-to-all(bf16[4,192,1024]{2,1,0:T(8,128)(2,1)S(1)} %bitcast.100), channel_id=1, replica_groups={{0,1,2,3},{4,5,6,7},{8,9,10,11},{12,13,14,15},{16,17,18,19},{20,21,22,2..., dimensions={0} | all-to-all | bytes 3145728 | tf_op jit(solution)/shard_map/all_to_all | solution.py:353
  567.8 33.1 %grad_far.1 = (f32[192,4096]{1,0:T(8,128)}, bf16[384,2048]{1,0:T(8,128)(2,1)}, bf16[384,2048]{1,0:T(8,128)(2,1)}) custom-call(s32[16,2]{1,0:T(8,128)} %copy.136.span, s32[1,4096]{1,0:T(1,128)} %bitcast.109, s32[8192,1]{1,0:T(8,128)} %fusion.2.ktag_ref, bf16[192,4096]{1,0:T(8,128)(2,1)} %fusion.1.qt_ref, bf16[192,4096]{1,0:T(8,128)(2,1)} %bitcast.98, ...), custom_call_target="tpu_custom_call" | custom-call | flops 2415919104 | bytes 20971520 | tf_op jit(solution)/shard_map/grad_far/pallas_call | solution.py:200
  600.9 33.8 %collective-permute-start.4 = (bf16[384,2048]{1,0:T(8,128)(2,1)}, bf16[384,2048]{1,0:T(8,128)(2,1)}, u32[]{:S(2)}, u32[]{:S(2)}) collective-permute-start(bf16[384,2048]{1,0:T(8,128)(2,1)} %get-tuple-element.27), channel_id=1, source_target_pairs={{0,4},{1,5},{2,6},{3,7},{4,8},{5,9},{6,10},{7,11},{8,12},{9,13},{1... | collective-permute-start | bytes 4718600 | tf_op jit(solution)/shard_map/ppermute | solution.py:363
  636.0 126.3 %grad_own.1 = (bf16[192,4096]{1,0:T(8,128)(2,1)}, f32[384,4096]{1,0:T(8,128)}) custom-call(s32[16,2]{1,0:T(8,128)} %copy.136.span, s32[1,4096]{1,0:T(1,128)} %bitcast.110, s32[8192,1]{1,0:T(8,128)} %fusion.2.ktag_ref, bf16[192,4096]{1,0:T(8,128)(2,1)} %fusion.1.qt_ref, bf16[192,4096]{1,0:T(8,128)(2,1)} %bitcast.99, ...), custom_call_target="tpu_custom_call" | custom-call | flops 12079595520 | bytes 20971520 | tf_op jit(solution)/shard_map/grad_own/pallas_call | solution.py:200
  769.1 13.2 %fusion.21 = f32[4096,768]{0,1:T(8,128)} fusion(bf16[768,576]{1,0:T(8,128)(2,1)} %bitcast.8, bf16[384,2048]{1,0:T(8,128)(2,1)S(1)} %get-tuple-element.131, bf16[384,2048]{1,0:T(8,128)(2,1)S(1)} %get-tuple-element.130, bf16[192,4096]{1,0:T(8,128)(2,1)S(1)} %copy-done.7), kind=kOutput, calls=%fused_computation.124 | convolution fusion | flops 3638034432 | bytes 18186240 | tf_op jit(solution)/shard_map/ct,dc->td/dot_general | solution.py:378
  782.3 9.2 convolution_bitcast_fusion
  794.3 21.8 %all-to-all-start.3 = ((f32[32,24,576]{2,1,0:T(8,128)}), f32[32,24,576]{2,1,0:T(8,128)}, u32[]{:S(2)}, u32[]{:S(2)}) async-start(f32[32,24,576]{2,1,0:T(8,128)} %bitcast.94), calls=%async_computation.4 | async-start | bytes 3932160 | tf_op jit(solution)/shard_map/all_to_all | solution.py:382
  823.5 59.8 %all-reduce.2 = f32[32,288]{1,0:T(8,128)S(1)} all-reduce(f32[32,288]{1,0:T(8,128)S(1)} %pad_maximum_fusion.4), channel_id=4, replica_groups=mesh['fsdp'=32] {'fsdp'}, use_global_device_ids=true, to_apply=%region_20.21.clone | all-reduce | flops 9216 | bytes 73728
  896.7 13.8 %reduce-scatter.3.cloned.1.call-done = f32[1024,768]{0,1:T(8,128)} async-done(((f32[4096,768]{0,1:T(8,128)}), f32[1024,768]{0,1:T(8,128)}) %reduce-scatter.3.cloned.1.call-update) | async-done | bytes 3145744 | tf_op jit(solution)/shard_map/reduce_scatter | solution.py:379
  (205 shorter events, 146.3 us)
Async XLA Ops:
  7.2 82.5 %all-gather.4.cloned.1.call-start = ((), (), s32[]{:S(2)}) async-start(), calls=%async_computation.6 | async-start | bytes 7864320 | tf_op jit(solution)/shard_map/all_gather | solution.py:289
  7.9 32.1 %copy-start.12 = (bf16[24]{0:T(256)(128)(2,1)S(1)}, bf16[24]{0:T(256)(128)(2,1)}, u32[]{:S(2)}) copy-start(bf16[24]{0:T(256)(128)(2,1)} %param.21) | copy-start | bytes 148
  7.9 32.1 %copy-start.13 = (bf16[24]{0:T(256)(128)(2,1)S(1)}, bf16[24]{0:T(256)(128)(2,1)}, u32[]{:S(2)}) copy-start(bf16[24]{0:T(256)(128)(2,1)} %param.22) | copy-start | bytes 148
  8.0 32.1 %copy-start.14 = (bf16[24]{0:T(256)(128)(2,1)S(1)}, bf16[24]{0:T(256)(128)(2,1)}, u32[]{:S(2)}) copy-start(bf16[24]{0:T(256)(128)(2,1)} %param.24) | copy-start | bytes 148
  8.0 32.1 %copy-start.15 = (bf16[24]{0:T(256)(128)(2,1)S(1)}, bf16[24]{0:T(256)(128)(2,1)}, u32[]{:S(2)}) copy-start(bf16[24]{0:T(256)(128)(2,1)} %param.25) | copy-start | bytes 148
  8.0 32.1 %copy-start.16 = (bf16[24]{0:T(256)(128)(2,1)S(1)}, bf16[24]{0:T(256)(128)(2,1)}, u32[]{:S(2)}) copy-start(bf16[24]{0:T(256)(128)(2,1)} %param.26) | copy-start | bytes 148
  8.0 32.1 %copy-start.17 = (bf16[24]{0:T(256)(128)(2,1)S(1)}, bf16[24]{0:T(256)(128)(2,1)}, u32[]{:S(2)}) copy-start(bf16[24]{0:T(256)(128)(2,1)} %param.30) | copy-start | bytes 148
  8.0 32.1 %copy-start.18 = (bf16[24]{0:T(256)(128)(2,1)S(1)}, bf16[24]{0:T(256)(128)(2,1)}, u32[]{:S(2)}) copy-start(bf16[24]{0:T(256)(128)(2,1)} %param.31) | copy-start | bytes 148
  8.0 32.1 %copy-start.19 = (bf16[24]{0:T(256)(128)(2,1)S(1)}, bf16[24]{0:T(256)(128)(2,1)}, u32[]{:S(2)}) copy-start(bf16[24]{0:T(256)(128)(2,1)} %param.32) | copy-start | bytes 148
  8.0 32.1 %copy-start.20 = (bf16[96]{0:T(256)(128)(2,1)S(1)}, bf16[96]{0:T(256)(128)(2,1)}, u32[]{:S(2)}) copy-start(bf16[96]{0:T(256)(128)(2,1)} %param.28) | copy-start | bytes 580
  8.0 423.5 %all-gather.6.cloned.1.call-start = ((), (), s32[]{:S(2)}) async-start(), calls=%async_computation.7 | async-start | bytes 10948608 | tf_op jit(solution)/shard_map/all_gather | solution.py:282
  13.7 95.1 %all-to-all-start = ((bf16[32,24,576]{2,1,0:T(8,128)(2,1)}), bf16[32,24,576]{2,1,0:T(8,128)(2,1)}, u32[]{:S(2)}, u32[]{:S(2)}) async-start(bf16[32,24,576]{2,1,0:T(8,128)(2,1)} %bitcast.7), calls=%async_computation | async-start | bytes 1966080 | tf_op jit(solution)/shard_map/all_to_all | solution.py:270
  35.7 48.5 %collective-permute-start = (s32[2048]{0:T(1024)S(1)}, s32[2048]{0:T(1024)S(1)}, u32[]{:S(2)}, u32[]{:S(2)}) collective-permute-start(s32[2048]{0:T(1024)S(1)} %get-tuple-element.152), channel_id=1, source_target_pairs={{0,4},{1,5},{2,6},{3,7},{4,8},{5,9},{6,10},{7,11},{8,12},{9,13},{1... | collective-permute-start | bytes 24584 | tf_op jit(solution)/shard_map/ppermute | solution.py:293
  38.7 45.5 %collective-permute-start.1 = (s32[2048]{0:T(1024)S(1)}, s32[2048]{0:T(1024)S(1)}, u32[]{:S(2)}, u32[]{:S(2)}) collective-permute-start(s32[2048]{0:T(1024)S(1)} %get-tuple-element.153), channel_id=1, source_target_pairs={{4,0},{5,1},{6,2},{7,3},{8,4},{9,5},{10,6},{11,7},{12,8},{13,9},{1... | collective-permute-start | bytes 24584 | tf_op jit(solution)/shard_map/ppermute | solution.py:294
  95.6 161.5 %collective-permute-start.2 = (bf16[2048,768]{1,0:T(8,128)(2,1)}, bf16[2048,768]{1,0:T(8,128)(2,1)S(1)}, u32[]{:S(2)}, u32[]{:S(2)}) collective-permute-start(bf16[2048,768]{1,0:T(8,128)(2,1)} %get-tuple-element.133), channel_id=1, source_target_pairs={{0,4},{1,5},{2,6},{3,7},{4,8},{5,9},{6,10},{7,11},{8,12},{9,13},{1... | collective-permute-start | bytes 9437192 | tf_op jit(solution)/shard_map/ppermute | solution.py:293
  101.1 160.9 %collective-permute-start.3 = (bf16[2048,768]{1,0:T(8,128)(2,1)}, bf16[2048,768]{1,0:T(8,128)(2,1)}, u32[]{:S(2)}, u32[]{:S(2)}) collective-permute-start(bf16[2048,768]{1,0:T(8,128)(2,1)} %get-tuple-element.132), channel_id=1, source_target_pairs={{4,0},{5,1},{6,2},{7,3},{8,4},{9,5},{10,6},{11,7},{12,8},{13,9},{1... | collective-permute-start | bytes 9437192 | tf_op jit(solution)/shard_map/ppermute | solution.py:294
  108.7 150.3 %slice-start = ((s8[6291456]{0:T(1024)(128)(4,1)}), s8[4194304]{0:T(1024)(128)(4,1)S(1)}, s32[]{:S(2)}) async-start(s8[6291456]{0:T(1024)(128)(4,1)} %bitcast.92), calls=%async_computation.10 | async-start | bytes 8388608
  108.7 150.3 %slice-start.1 = ((s8[6291456]{0:T(1024)(128)(4,1)}), s8[2097152]{0:T(1024)(128)(4,1)S(1)}, s32[]{:S(2)}) async-start(s8[6291456]{0:T(1024)(128)(4,1)} %bitcast.92), calls=%async_computation.11 | async-start | bytes 4194304
  407.0 24.6 %all-to-all-start.1 = ((bf16[192,4,1024]{2,0,1:T(8,128)(2,1)}), bf16[192,4,1024]{2,0,1:T(8,128)(2,1)}, u32[]{:S(2)}, u32[]{:S(2)}) async-start(bf16[192,4,1024]{2,0,1:T(8,128)(2,1)} %bitcast.91), calls=%async_computation.1 | async-start | bytes 3145728 | tf_op jit(solution)/shard_map/all_to_all | solution.py:320
  411.5 481.2 %reduce-scatter.5.cloned.1.call-start = ((), (), s32[]{:S(2)}) async-start(), calls=%async_computation.9 | async-start | bytes 10948608 | tf_op jit(solution)/shard_map/reduce_scatter | solution.py:351
  538.9 371.6 %reduce-scatter.3.cloned.1.call-start = ((), (), s32[]{:S(2)}) async-start(), calls=%async_computation.8 | async-start | bytes 15728640 | tf_op jit(solution)/shard_map/reduce_scatter | solution.py:379
  600.9 161.4 %collective-permute-start.4 = (bf16[384,2048]{1,0:T(8,128)(2,1)}, bf16[384,2048]{1,0:T(8,128)(2,1)}, u32[]{:S(2)}, u32[]{:S(2)}) collective-permute-start(bf16[384,2048]{1,0:T(8,128)(2,1)} %get-tuple-element.27), channel_id=1, source_target_pairs={{0,4},{1,5},{2,6},{3,7},{4,8},{5,9},{6,10},{7,11},{8,12},{9,13},{1... | collective-permute-start | bytes 4718600 | tf_op jit(solution)/shard_map/ppermute | solution.py:363
  634.8 127.6 %collective-permute-start.5 = (bf16[384,2048]{1,0:T(8,128)(2,1)}, bf16[384,2048]{1,0:T(8,128)(2,1)}, u32[]{:S(2)}, u32[]{:S(2)}) collective-permute-start(bf16[384,2048]{1,0:T(8,128)(2,1)} %get-tuple-element.28), channel_id=1, source_target_pairs={{4,0},{5,1},{6,2},{7,3},{8,4},{9,5},{10,6},{11,7},{12,8},{13,9},{1... | collective-permute-start | bytes 4718600 | tf_op jit(solution)/shard_map/ppermute | solution.py:362
  794.3 90.2 %all-to-all-start.3 = ((f32[32,24,576]{2,1,0:T(8,128)}), f32[32,24,576]{2,1,0:T(8,128)}, u32[]{:S(2)}, u32[]{:S(2)}) async-start(f32[32,24,576]{2,1,0:T(8,128)} %bitcast.94), calls=%async_computation.4 | async-start | bytes 3932160 | tf_op jit(solution)/shard_map/all_to_all | solution.py:382
  (12 other events, 92.1 us)
Sparse Core Ops, SparseCore 0:
  9.6 60.3 all-gather.3
  72.9 162.6 all-gather.5
  539.0 210.5 reduce-scatter.4
  782.4 128.0 reduce-scatter.2

commit v2 on v1

--- a/solution.py
+++ b/solution.py
@@ -231,6 +231,253 @@
     )(*args)
 
 
+MESH = pl.DeviceIdType.MESH
+CHUNKS = 4
+MESSAGE_ROWS = 32
+W_LANES = 640
+KV_AT = 256
+
+
+def remote(src, dst, send, recv, target):
+    return pltpu.make_async_remote_copy(
+        src_ref=src,
+        dst_ref=dst,
+        send_sem=send,
+        recv_sem=recv,
+        device_id=(target,),
+        device_id_type=MESH,
+    )
+
+
+def share_kernel(
+    n_dev, tok_ref, code_ref, w_ref, x_out, c_out, w_out,
+    w_send, w_recv, c_send, c_recv, part_send, part_recv, mate_send, mate_recv,
+    up_send, up_recv, down_send, down_recv, cross_send, cross_recv,
+    fwd_send, fwd_recv, keep_sem,
+):
+    n_group = n_dev // GROUP
+    me = lax.axis_index("fsdp")
+    g = me // GROUP
+    s = me % GROUP
+    k = s % 2
+    hi = s // 2
+    partner = me + 1 - 2 * k
+    mate = me + 2 - 4 * hi
+    mate_block = 4 + k - 2 * hi
+    has_up = g < n_group - 1
+    has_down = g > 0
+    rows = tok_ref.shape[0] // CHUNKS
+    half = CHUNKS // 2
+
+    barrier = pltpu.get_barrier_semaphore()
+
+    def greet(r, carry):
+        pl.semaphore_signal(
+            barrier, inc=1, device_id=(lax.rem(me + r, n_dev),), device_id_type=MESH
+        )
+        return carry
+
+    lax.fori_loop(1, n_dev, greet, 0)
+    pl.semaphore_wait(barrier, n_dev - 1)
+
+    def chunk(ref, c):
+        return ref.at[pl.ds(pl.multiple_of(c * rows, rows), rows)]
+
+    def spot(b, c):
+        return x_out.at[b, pl.ds(pl.multiple_of(c * rows, rows), rows)]
+
+    def to_partner(c):
+        return remote(chunk(tok_ref, c), spot(2 + s, c), part_send.at[c], part_recv.at[c], partner)
+
+    def to_mate(c):
+        return remote(chunk(tok_ref, c), spot(2 + s, c), mate_send.at[c], mate_recv.at[c], mate)
+
+    def up_own(c):
+        return remote(chunk(tok_ref, c), spot(k, c), up_send.at[c], up_recv.at[c], me + GROUP)
+
+    def up_mate(c):
+        return remote(spot(mate_block, c), spot(k, c), up_send.at[c], up_recv.at[c], me + GROUP)
+
+    def down_own(c):
+        return remote(
+            chunk(tok_ref, c), spot(6 + k, c), down_send.at[c], down_recv.at[c], me - GROUP
+        )
+
+    def down_mate(c):
+        return remote(
+            spot(mate_block, c + half), spot(6 + k, c + half), down_send.at[c], down_recv.at[c],
+            me - GROUP,
+        )
+
+    def cross(c):
+        at = c + half * hi
+        return remote(spot(6 + k, at), spot(6 + k, at), cross_send.at[c], cross_recv.at[c], mate)
+
+    def forward(b, c, slot):
+        return remote(spot(b, c), spot(b, c), fwd_send.at[slot], fwd_recv.at[slot], partner)
+
+    keep_x = pltpu.make_async_copy(tok_ref, x_out.at[2 + s], keep_sem.at[0])
+    keep_c = pltpu.make_async_copy(code_ref, c_out.at[2 + s], keep_sem.at[1])
+    keep_w = pltpu.make_async_copy(w_ref.at[s], w_out.at[me], keep_sem.at[2])
+    keep_x.start()
+    keep_c.start()
+    keep_w.start()
+
+    def w_copy(r):
+        target = lax.rem(me + r, n_dev)
+        return remote(
+            w_ref.at[lax.rem(target, GROUP)], w_out.at[me], w_send.at[r], w_recv.at[r], target
+        )
+
+    def w_start(r, carry):
+        w_copy(r).start()
+        return carry
+
+    def c_group(j):
+        target = GROUP * g + lax.rem(s + j, GROUP)
+        return remote(code_ref, c_out.at[2 + s], c_send.at[j], c_recv.at[2 + s], target)
+
+    def c_far(j):
+        step = GROUP * (2 * hi - 1)
+        b = 6 + s - 8 * hi
+        target = GROUP * g + step + j
+        return remote(code_ref, c_out.at[b], c_send.at[GROUP + j], c_recv.at[b], target)
+
+    sends_far = jnp.where(hi == 1, g < n_group - 1, g > 0)
+    for j in range(1, GROUP):
+        c_group(j).start()
+
+    @pl.when(sends_far)
+    def _():
+        for j in range(GROUP):
+            c_far(j).start()
+
+    for c in range(CHUNKS):
+        to_mate(c).start()
+        to_partner(c).start()
+
+        @pl.when((hi == 1) & has_up)
+        def _():
+            up_own(c).start()
+
+        if c < half:
+
+            @pl.when((hi == 0) & has_down)
+            def _():
+                down_own(c).start()
+
+    lax.fori_loop(1, n_dev, w_start, 0)
+
+    for c in range(CHUNKS):
+        to_mate(c).wait_recv()
+        forward(mate_block, c, c).start()
+
+        @pl.when((hi == 0) & has_up)
+        def _():
+            up_mate(c).start()
+
+        if c >= half:
+
+            @pl.when((hi == 1) & has_down)
+            def _():
+                down_mate(c - half).start()
+
+    @pl.when(has_up)
+    def _():
+        for c in range(half):
+            down_own(c).wait_recv()
+            cross(c).start()
+            forward(6 + k, c + half * hi, 2 * CHUNKS + c).start()
+
+    @pl.when(has_down)
+    def _():
+        for c in range(CHUNKS):
+            up_own(c).wait_recv()
+            forward(k, c, CHUNKS + c).start()
+
+    @pl.when(has_up)
+    def _():
+        for c in range(half):
+            cross(c).wait_recv()
+            forward(6 + k, c + half * (1 - hi), 2 * CHUNKS + half + c).start()
+
+    for c in range(CHUNKS):
+        to_partner(c).wait()
+        to_mate(c).wait_send()
+        forward(mate_block, c, c).wait()
+
+    @pl.when(has_down)
+    def _():
+        for c in range(CHUNKS):
+            forward(k, c, CHUNKS + c).wait()
+        for c in range(half):
+            down_own(c).wait_send()
+
+    @pl.when(has_up)
+    def _():
+        for c in range(half):
+            cross(c).wait_send()
+            forward(6 + k, c, 2 * CHUNKS + c).wait()
+            forward(6 + k, c, 2 * CHUNKS + half + c).wait()
+        for c in range(CHUNKS):
+            up_own(c).wait_send()
+
+    for j in range(1, GROUP):
+        c_group(j).wait_send()
+        remote(
+            code_ref, c_out.at[0], c_send.at[j], c_recv.at[2 + lax.rem(s + j, GROUP)], partner
+        ).wait_recv()
+
+    @pl.when(sends_far)
+    def _():
+        for j in range(GROUP):
+            c_far(j).wait_send()
+
+    @pl.when(has_down)
+    def _():
+        for b in range(2):
+            remote(code_ref, c_out.at[b], c_send.at[0], c_recv.at[b], partner).wait_recv()
+
+    @pl.when(has_up)
+    def _():
+        for b in range(6, 8):
+            remote(code_ref, c_out.at[b], c_send.at[0], c_recv.at[b], partner).wait_recv()
+
+    def w_wait(r, carry):
+        w_copy(r).wait()
+        return carry
+
+    lax.fori_loop(1, n_dev, w_wait, 0)
+    keep_x.wait()
+    keep_c.wait()
+    keep_w.wait()
+
+
+def share(n_dev, tokens, code, w_send):
+    vmem = pl.BlockSpec(memory_space=pltpu.VMEM)
+    anywhere = pl.BlockSpec(memory_space=pl.ANY)
+    dma = lambda n: pltpu.SemaphoreType.DMA((n,))
+    half = CHUNKS // 2
+    return pl.pallas_call(
+        functools.partial(share_kernel, n_dev),
+        in_specs=[vmem] * 3,
+        out_specs=[anywhere] * 3,
+        out_shape=[
+            jax.ShapeDtypeStruct((8,) + tokens.shape, tokens.dtype),
+            jax.ShapeDtypeStruct((8,) + code.shape, code.dtype),
+            jax.ShapeDtypeStruct((n_dev,) + w_send.shape[1:], w_send.dtype),
+        ],
+        scratch_shapes=[
+            dma(n_dev), dma(n_dev), dma(2 * GROUP), dma(8),
+            dma(CHUNKS), dma(CHUNKS), dma(CHUNKS), dma(CHUNKS),
+            dma(CHUNKS), dma(CHUNKS), dma(half), dma(half), dma(half), dma(half),
+            dma(3 * CHUNKS), dma(3 * CHUNKS), dma(3),
+        ],
+        compiler_params=pltpu.CompilerParams(collective_id=0, has_side_effects=True),
+        name="share",
+    )(tokens, code, w_send)
+
+
 def body(
     n_dev,
     tokens,
@@ -259,43 +506,49 @@
     place = me % GROUP
     group_id = me // GROUP
     n_group = n_dev // GROUP
+    up = [(i, i + GROUP) for i in range(n_dev - GROUP)]
+    down = [(i + GROUP, i) for i in range(n_dev - GROUP)]
     groups = [[GROUP * g + j for j in range(GROUP)] for g in range(n_group)]
 
     wq = w_qkv[:, :D].reshape(rows_w, GROUP, Q_ROWS)
     wk = w_qkv[:, D : 2 * D].reshape(rows_w, GROUP, OWN_HEADS, 1, HEAD_DIM)
     wv = w_qkv[:, 2 * D :].reshape(rows_w, GROUP, OWN_HEADS, 1, HEAD_DIM)
     wkv = jnp.concatenate([wk, wv], axis=3).reshape(rows_w, GROUP, KV_ROWS)
-    w_cut = jnp.concatenate([wq, wkv], axis=2).transpose(1, 0, 2)
-    w_send = jnp.tile(w_cut, (n_group, 1, 1))
-    w_mix = lax.all_to_all(w_send, "fsdp", 0, 0, tiled=True).reshape(D, MIX_ROWS)
+    gap = jnp.zeros((rows_w, GROUP, KV_AT - Q_ROWS), bf16)
+    w_cut = jnp.concatenate([wq, gap, wkv], axis=2).transpose(1, 0, 2)
     small = jnp.concatenate(
         [bias_query, bias_value, bias_out, gain_one, shift_one, bias_down, gain_two, shift_two, bias_up]
     )
-    small_all = lax.all_gather(small, "fsdp", axis=0, tiled=False)
+    n_small = small.shape[0]
+    small_rows = jnp.pad(small[None], ((0, MESSAGE_ROWS - rows_w - 1), (0, W_LANES - n_small)))
+    small_rows = jnp.broadcast_to(small_rows[None], (GROUP,) + small_rows.shape)
+    w_send = jnp.concatenate([w_cut, small_rows], axis=1)
+    big = jnp.concatenate([w_out, w_up, w_down.reshape(rows_w, -1)], axis=1)
+    big_all = lax.all_gather(big, "fsdp", axis=0, tiled=True)
+    ff = w_up.shape[1]
+    wo_full = big_all[:, :D]
+    wu_full = big_all[:, D : D + ff]
+    wd_full = big_all[:, D + ff :].reshape(ff, D)
+
+    code = (segment_ids * 2 + pad_mask).reshape(8, row_count // 8)
+    x_win, code_win, w_got = share(n_dev, tokens, code, w_send)
+    x_win = x_win.reshape(window, D)
+    x_own = x_win[LEN_MAX : LEN_MAX + own]
+    code_win = code_win.reshape(window)
+    at = jnp.arange(window)
+    code_win = jnp.where((group_id == 0) & (at < LEN_MAX), -2, code_win)
+    code_win = jnp.where(
+        (group_id == n_group - 1) & (at >= LEN_MAX + own), 2 * n_dev * row_count, code_win
+    )
+    code_own = code_win[LEN_MAX : LEN_MAX + own]
+    w_mix = w_got[:, :rows_w].reshape(D, W_LANES)
+    small_all = w_got[:, rows_w, :n_small]
     rows8 = small_all[:, : 8 * rows_w].reshape(n_dev, 8, rows_w).transpose(1, 0, 2).reshape(8, D)
     rows8 = rows8.astype(f32)
     bu_full = small_all[:, 8 * rows_w :].reshape(-1).astype(f32)
     bq_full, bv_full, bo_full, g1_full, s1_full, bd_full, g2_full, s2_full = [
         rows8[j] for j in range(8)
     ]
-    big = jnp.concatenate([w_out, w_up, w_down.reshape(rows_w, -1)], axis=1)
-    big_all = lax.all_gather(big, "fsdp", axis=0, tiled=True)
-    ff = w_up.shape[1]
-    wo_full = big_all[:, :D]
-    wu_full = big_all[:, D : D + ff]
-    wd_full = big_all[:, D + ff :].reshape(ff, D)
-
-    code = segment_ids * 2 + pad_mask
-    x_own = lax.all_gather(tokens, "fsdp", axis=0, tiled=True, axis_index_groups=groups)
-    code_own = lax.all_gather(code, "fsdp", axis=0, tiled=True, axis_index_groups=groups)
-    up = [(i, i + GROUP) for i in range(n_dev - GROUP)]
-    down = [(i + GROUP, i) for i in range(n_dev - GROUP)]
-    x_left, c_left = lax.ppermute((x_own[own - LEN_MAX :], code_own[own - LEN_MAX :]), "fsdp", up)
-    x_right, c_right = lax.ppermute((x_own[:LEN_MAX], code_own[:LEN_MAX]), "fsdp", down)
-    x_win = jnp.concatenate([x_left, x_own, x_right], axis=0)
-    c_left = jnp.where(group_id == 0, -2, c_left)
-    c_right = jnp.where(group_id == n_group - 1, 2 * n_dev * row_count, c_right)
-    code_win = jnp.concatenate([c_left, code_own, c_right])
     seg_win = code_win >> 1
     ktag = jnp.where((code_win & 1) == 1, seg_win + 1, 0).reshape(window, 1)
     seg_own = code_own >> 1
@@ -309,7 +562,8 @@
     bq = lax.dynamic_slice(bq_full, (place * Q_ROWS,), (Q_ROWS,))
     bv = lax.dynamic_slice(bv_full, (place * Q_ROWS,), (Q_ROWS,)).reshape(OWN_HEADS, 1, HEAD_DIM)
     bkv = jnp.concatenate([jnp.zeros_like(bv), bv], axis=1).reshape(KV_ROWS)
-    w_q, w_kv = w_mix[:, :Q_ROWS], w_mix[:, Q_ROWS:]
+    w_q, w_kv = w_mix[:, :Q_ROWS], w_mix[:, KV_AT:]
+    w_mix = jnp.concatenate([w_q, w_kv], axis=1)
     qt = jnp.einsum("dc,td->ct", w_q, x_own, preferred_element_type=f32) + bq[:, None]
     qt = qt.astype(bf16) * jnp.asarray(score_scale, bf16)
     kv = (jnp.dot(x_win, w_kv, preferred_element_type=f32) + bkv).astype(bf16)

time: 923 us -> 824 us (0.89); the launches traced: 925 us -> 815 us
  waiting for transfers between devices: 173 us -> 27.8 us
  Pallas kernels: 276 us -> 382 us
  blocking collectives: 139 us -> 82.2 us
  starting transfers between devices: 79.4 us -> 50.9 us
    ppermute x4 -> x0, waiting for transfers between devices: 142 us -> none  [the longest x2 142 us: body(): lax.ppermute((x_own[own - LEN_MAX:], code_own[own - LEN_MAX:]), 'fsdp', up)]
    pallas_call x0 -> x1, Pallas kernels: none -> 97 us  [share(): pl.pallas_call(functools.partial(share_kernel, n_dev), in_specs=[vmem] *...]
    unnamed x2 -> x1, blocking collectives: 102 us -> 59.8 us
    ppermute x1, starting transfers between devices: 33.8 us -> 16.9 us  [body(): from_left = lax.ppermute(dkv_right, 'fsdp', up)]
    all_gather x1 -> x0, blocking collectives: 14.5 us -> none  [body(): lax.all_gather(code, 'fsdp', axis=0, tiled=True, axis_index_groups=groups)]
    ppermute x4 -> x0, starting transfers between devices: 10.2 us -> none  [the longest x2 7.43 us: body(): lax.ppermute((x_own[own - LEN_MAX:], code_own[own - LEN_MAX:]), 'fsdp', up)]
    unnamed x62 -> x59, local copies, waits for them, and re-layouts: 20.1 us -> 16.7 us
  transfers between devices with their start and end apart: 13 -> 7, of which waited for: 3 -> 2; matrix products, arithmetic and copies ran while one was open for 14% -> 16% of each run, Pallas kernels for 30% -> 47%
where the time goes in v2:
time: 824 us; the launch traced here: 815 us
  Pallas kernels  382 us (46%)
  matrix products  127 us (15%)
  local copies, waits for them, and re-layouts  90.7 us (11%)
  blocking collectives  82.2 us (10%)
  starting transfers between devices  50.9 us (6%)
  other arithmetic  39.6 us (5%)
  waiting for transfers between devices  27.8 us (3%)
  between operations  15 us (2%)
    pallas_call x2, Pallas kernels, attend_grad(): pl.pallas_call(functools.partial(grad_kernel, parts, final), grid_spec=pl...  165 us
    pallas_call x1, Pallas kernels, attend(): pl.pallas_call(attend_kernel, grid_spec=pltpu.PrefetchScalarGridSpec(num_...  121 us
    pallas_call x1, Pallas kernels, share(): pl.pallas_call(functools.partial(share_kernel, n_dev), in_specs=[vmem] *...  97 us
    unnamed x1, blocking collectives  59.8 us
    all_to_all x1, starting transfers between devices, body(): lax.all_to_all(d_w_mix.reshape(n_dev, rows_w, MIX_ROWS), 'fsdp', 0, 0, ti...  27.9 us
    all_to_all x1, blocking collectives, body(): lax.all_to_all(dctx_t.reshape(GROUP, Q_ROWS, row_count), 'fsdp', 0, 2, ax...  22.5 us
    dot_general x1, matrix products, body(): jnp.einsum('dc,td->ct', w_kv, x_win, preferred_element_type=f32)  19.4 us
    ppermute x1, starting transfers between devices, body(): from_left = lax.ppermute(dkv_right, 'fsdp', up)  16.9 us
  transfers between devices with their start and end apart: 7, of which 2 were waited for; matrix products, arithmetic and copies ran while one was open for 16% of the time, Pallas kernels for 47%

profile of v2, /device:TPU:0, one launch (start us, length us, event | category | flops | bytes accessed | tf_op | source)
XLA Modules:
  0.0 815.2 jit_solution(16674702172774139213)
XLA Ops:
  19.3 97.0 %share.1 = (bf16[8,1024,768]{2,1,0:T(8,128)(2,1)}, s32[8,8,128]{2,1,0:T(8,128)}, bf16[32,32,640]{2,1,0:T(8,128)(2,1)}) custom-call(bf16[1024,768]{1,0:T(8,128)(2,1)} %tok_ref.1, s32[8,128]{1,0:T(8,128)} %add_bitcast_fusion.code_ref, bf16[4,32,640]{2,1,0:T(8,128)(2,1)} %pad_maximum_fusion.4.w_ref), custom_call_target="tpu_custom_call" | custom-call | tf_op jit(solution)/shard_map/share/pallas_call | solution.py:461
  137.3 19.4 %add_convert_fusion.1.kvt_ref = bf16[384,8192]{1,0:T(8,128)(2,1)} fusion(bf16[8192,768]{1,0:T(8,128)(2,1)} %bitcast.113, f32[384]{0:T(512)S(1)} %add.194, bf16[768,640]{1,0:T(8,128)(2,1)S(1)} %bitcast.109), kind=kOutput, calls=%fused_computation.4 | convolution fusion | flops 4838129664 | bytes 19466240 | tf_op jit(solution)/shard_map/dc,td->ct/dot_general | solution.py:570
  156.8 8.7 %add_convert_fusion.2.kv_ref = bf16[8192,384]{1,0:T(8,128)(2,1)} fusion(bf16[8192,768]{1,0:T(8,128)(2,1)S(1)} %bitcast.116, f32[384]{0:T(512)S(1)} %add.194, bf16[768,640]{1,0:T(8,128)(2,1)S(1)} %bitcast.110), kind=kOutput, calls=%fused_computation.5 | convolution fusion | flops 4838129664 | bytes 19466240 | tf_op jit(solution)/shard_map/dot_general | solution.py:569
  168.4 120.6 %attend.1 = (bf16[192,4096]{1,0:T(8,128)(2,1)}, f32[8,4096]{1,0:T(8,128)}) custom-call(s32[16,2]{1,0:T(8,128)} %copy.103.span, s32[1,4096]{1,0:T(1,128)} %bitcast.128, s32[8192,1]{1,0:T(8,128)} %add_select_fusion.ktag_ref, bf16[192,4096]{1,0:T(8,128)(2,1)} %fusion.1.qt_ref, bf16[8192,384]{1,0:T(8,128)(2,1)} %add_convert_fusion.2.kv_ref, ...), custom_call_target="tpu_custom_call" | custom-call | flops 6442450944 | bytes 20971520 | tf_op jit(solution)/shard_map/attend/pallas_call | solution.py:94
  300.5 16.1 %all-to-all-done = bf16[192,4,1024]{2,0,1:T(8,128)(2,1)} async-done(((bf16[192,4,1024]{2,0,1:T(8,128)(2,1)}), bf16[192,4,1024]{2,0,1:T(8,128)(2,1)}, u32[]{:S(2)}, u32[]{:S(2)}) %all-to-all-start) | async-done | bytes 1572896 | tf_op jit(solution)/shard_map/all_to_all | solution.py:574
  326.3 8.5 %reshape.415 = bf16[3072,768]{1,0:T(8,128)(2,1)} reshape(bf16[768,3072]{1,0:T(8,128)(2,1)} %slice.246) | data formatting | bytes 9437184 | tf_op jit(solution)/shard_map/reshape | solution.py:531
  334.8 11.1 %multiply_convert_fusion = (bf16[1024,3072]{1,0:T(8,128)(2,1)}, f32[1024,3072]{1,0:T(8,128)S(1)}) fusion(f32[3072]{0:T(1024)S(1)} %reshape.426, bf16[768,6912]{1,0:T(8,128)(2,1)} %all-gather.2.cloned.1.call-done, f32[1024,768]{0,1:T(8,128)S(1)} %get-tuple-element.144, f32[768]{0:T(1024)S(1)} %add.204, f32[768]{0:T(1024)S(1)} %mul.166, f32[1024]{0:T(1024)S(1)} %fusion.26, ...), kind=kOutput, calls=%fused_computation.2 | convolution fusion | flops 4854644736 | bytes 26765312 | tf_op jit(solution)/shard_map/dot_general | solution.py:582
  345.9 8.6 %fusion.41 = (f32[1024]{0:T(1024)S(1)}, f32[1024,768]{0,1:T(8,128)S(1)}) fusion(f32[768]{0:T(1024)S(1)} %add.211, bf16[1024,3072]{1,0:T(8,128)(2,1)} %get-tuple-element.145, bf16[3072,768]{1,0:T(8,128)(2,1)S(1)} %copy-done.8, f32[768]{0:T(1024)S(1)} %add.204, f32[768]{0:T(1024)S(1)} %mul.166, f32[1024]{0:T(1024)S(1)} %fusion.26, ...), kind=kOutput, calls=%fused_computation.141 | convolution fusion | flops 4837342208 | bytes 17323008 | tf_op jit(solution)/shard_map/dot_general | solution.py:585
  360.0 7.0 convolution_convert_fusion
  367.0 12.8 %convert_reduce_fusion = (f32[3072]{0:T(1024)S(1)}, bf16[1024,3072]{1,0:T(8,128)(2,1)S(1)}) fusion(bf16[1024,768]{0,1:T(8,128)(2,1)S(1)} %get-tuple-element.114, bf16[3072,768]{1,0:T(8,128)(2,1)S(1)} %copy-done.8, f32[1024,3072]{1,0:T(8,128)S(1)} %get-tuple-element.146, f32[3072]{0:T(1024)S(1)} %reshape.426), kind=kOutput, calls=%fused_computation | convolution fusion | flops 4882166784 | bytes 25190400 | tf_op jit(solution)/shard_map/rd,fd->rf/dot_general | solution.py:592
  382.4 7.0 convolution_convert_fusion.1
  389.4 8.5 %reshape.424 = bf16[768,3072]{1,0:T(8,128)(2,1)} reshape(bf16[3072,768]{1,0:T(8,128)(2,1)} %convolution_convert_fusion) | data formatting | bytes 9437184 | tf_op jit(solution)/shard_map/reshape | solution.py:603
  397.9 11.9 %multiply_reduce_fusion = (f32[768]{0:T(1024)S(1)}, f32[1024]{0:T(1024)S(1)}, f32[768]{0:T(1024)S(1)}, f32[1024,768]{0,1:T(8,128)S(1)}) fusion(f32[1024,768]{0,1:T(8,128)} %copy-done.2, f32[1024]{0:T(1024)S(1)} %fusion.26, f32[1024]{0:T(1024)S(1)} %broadcast_multiply_fusion.1, f32[768]{0:T(1024)S(1)} %mul.166, bf16[1024,3072]{1,0:T(8,128)(2,1)} %copy-done.17, ...), kind=kOutput, calls=%fused_computation.36 | convolution fusion | flops 4845204480 | bytes 22061056 | tf_op jit(solution)/shard_map/rf,df->rd/dot_general | solution.py:596
  418.3 9.1 %pad_maximum_fusion = bf16[768,6912]{1,0:T(8,128)(2,1)} fusion(bf16[768,3072]{1,0:T(8,128)(2,1)} %reshape.424, bf16[768,3072]{1,0:T(8,128)(2,1)} %convolution_convert_fusion.1, bf16[768,768]{1,0:T(8,128)(2,1)} %copy.116), kind=kLoop, calls=%fused_computation.6 | loop fusion | flops 31850496 | bytes 21233664 | tf_op jit(solution)/shard_map/concatenate | solution.py:602
  430.7 22.5 %all_to_all.35 = bf16[4,192,1024]{2,1,0:T(8,128)(2,1)S(1)} all-to-all(bf16[4,192,1024]{2,1,0:T(8,128)(2,1)S(1)} %bitcast.120), channel_id=1, replica_groups={{0,1,2,3},{4,5,6,7},{8,9,10,11},{12,13,14,15},{16,17,18,19},{20,21,22,2..., dimensions={0} | all-to-all | bytes 3145728 | tf_op jit(solution)/shard_map/all_to_all | solution.py:607
  456.2 38.4 %grad_far.1 = (f32[192,4096]{1,0:T(8,128)}, bf16[384,2048]{1,0:T(8,128)(2,1)}, bf16[384,2048]{1,0:T(8,128)(2,1)}) custom-call(s32[16,2]{1,0:T(8,128)} %copy.103.span, s32[1,4096]{1,0:T(1,128)} %bitcast.129, s32[8192,1]{1,0:T(8,128)} %add_select_fusion.ktag_ref, bf16[192,4096]{1,0:T(8,128)(2,1)} %fusion.1.qt_ref, bf16[192,4096]{1,0:T(8,128)(2,1)} %bitcast.118, ...), custom_call_target="tpu_custom_call" | custom-call | flops 2415919104 | bytes 20971520 | tf_op jit(solution)/shard_map/grad_far/pallas_call | solution.py:200
  494.6 16.9 %collective-permute-start = (bf16[384,2048]{1,0:T(8,128)(2,1)}, bf16[384,2048]{1,0:T(8,128)(2,1)}, u32[]{:S(2)}, u32[]{:S(2)}) collective-permute-start(bf16[384,2048]{1,0:T(8,128)(2,1)} %get-tuple-element.33), channel_id=1, source_target_pairs={{0,4},{1,5},{2,6},{3,7},{4,8},{5,9},{6,10},{7,11},{8,12},{9,13},{1... | collective-permute-start | bytes 4718600 | tf_op jit(solution)/shard_map/ppermute | solution.py:617
  515.7 126.2 %grad_own.1 = (bf16[192,4096]{1,0:T(8,128)(2,1)}, f32[384,4096]{1,0:T(8,128)}) custom-call(s32[16,2]{1,0:T(8,128)} %copy.103.span, s32[1,4096]{1,0:T(1,128)} %bitcast.130, s32[8192,1]{1,0:T(8,128)} %add_select_fusion.ktag_ref, bf16[192,4096]{1,0:T(8,128)(2,1)} %fusion.1.qt_ref, bf16[192,4096]{1,0:T(8,128)(2,1)} %bitcast.119, ...), custom_call_target="tpu_custom_call" | custom-call | flops 12079595520 | bytes 20971520 | tf_op jit(solution)/shard_map/grad_own/pallas_call | solution.py:200
  648.7 12.2 %fusion.19 = f32[4096,768]{0,1:T(8,128)} fusion(bf16[768,384]{1,0:T(8,128)(2,1)S(1)} %copy-done.13, bf16[768,192]{1,0:T(8,128)(2,1)S(1)} %slice.235, bf16[384,2048]{1,0:T(8,128)(2,1)S(1)} %get-tuple-element.122, bf16[384,2048]{1,0:T(8,128)(2,1)S(1)} %get-tuple-element.121, bf16[192,4096]{1,0:T(8,128)(2,1)S(1)} %copy-done.11), kind=kOutput, calls=%fused_computation.57 | convolution fusion | flops 3639803904 | bytes 18186240 | tf_op jit(solution)/shard_map/ct,dc->td/dot_general | solution.py:632
  661.0 8.9 %copy.111 = bf16[768,4096]{1,0:T(8,128)(2,1)} copy(bf16[768,4096]{0,1:T(8,128)(2,1)} %bitcast.104) | data formatting | bytes 12582912 | tf_op jit(solution)/shard_map/td,ct->dc/dot_general | solution.py:631
  669.9 10.5 %fusion.2 = f32[32,24,576]{2,1,0:T(8,128)} fusion(bf16[32,24,4096]{2,1,0:T(8,128)(2,1)} %bitcast.105, bf16[384,2048]{1,0:T(8,128)(2,1)} %copy-done.7, bf16[384,2048]{1,0:T(8,128)(2,1)} %copy-done.6, bf16[192,4096]{1,0:T(8,128)(2,1)} %get-tuple-element.31), kind=kOutput, calls=%fused_computation.19 | convolution fusion | flops 3638034432 | bytes 12779520 | tf_op jit(solution)/shard_map/td,ct->dc/dot_general | solution.py:631
  680.4 27.9 %all-to-all-start.2 = ((f32[32,24,576]{2,1,0:T(8,128)}), f32[32,24,576]{2,1,0:T(8,128)}, u32[]{:S(2)}, u32[]{:S(2)}) async-start(f32[32,24,576]{2,1,0:T(8,128)} %fusion.2), calls=%async_computation.3 | async-start | bytes 3932160 | tf_op jit(solution)/shard_map/all_to_all | solution.py:636
  715.7 59.8 %all-reduce.2 = f32[32,288]{1,0:T(8,128)S(1)} all-reduce(f32[32,288]{1,0:T(8,128)S(1)} %pad_maximum_fusion.5), channel_id=3, replica_groups=mesh['fsdp'=32] {'fsdp'}, use_global_device_ids=true, to_apply=%region_20.21.clone | all-reduce | flops 9216 | bytes 73728
  788.8 11.7 %reduce-scatter.3.cloned.1.call-done = f32[1024,768]{0,1:T(8,128)} async-done(((f32[4096,768]{0,1:T(8,128)}), f32[1024,768]{0,1:T(8,128)}) %reduce-scatter.3.cloned.1.call-update) | async-done | bytes 3145744 | tf_op jit(solution)/shard_map/reduce_scatter | solution.py:633
  (190 shorter events, 118.9 us)
Async XLA Ops:
  7.2 11.5 %copy-start.16 = (s32[1024]{0:T(1024)S(1)}, s32[1024]{0:T(1024)}, u32[]{:S(2)}) copy-start(s32[1024]{0:T(1024)} %param.18) | copy-start | bytes 12292
  7.2 11.5 %copy-start.15 = (s32[1024]{0:T(1024)S(1)}, s32[1024]{0:T(1024)}, u32[]{:S(2)}) copy-start(s32[1024]{0:T(1024)} %param.19) | copy-start | bytes 12292
  7.2 309.4 %all-gather.2.cloned.1.call-start = ((), (), s32[]{:S(2)}) async-start(), calls=%async_computation.5 | async-start | bytes 10948608 | tf_op jit(solution)/shard_map/all_gather | solution.py:527
  118.6 38.2 %copy-start.9 = (bf16[32,24,640]{2,1,0:T(8,128)(2,1)}, bf16[32,24,640]{2,1,0:T(8,128)(2,1)S(1)}, u32[]{:S(2)}) copy-start(bf16[32,24,640]{2,1,0:T(8,128)(2,1)S(1)} %slice.183) | copy-start | bytes 2949124
  121.2 6.9 copy-start.14
  130.8 26.0 %slice-start = ((s8[12582912]{0:T(1024)(128)(4,1)}), s8[4194304]{0:T(1024)(128)(4,1)S(1)}, s32[]{:S(2)}) async-start(s8[12582912]{0:T(1024)(128)(4,1)} %bitcast.114), calls=%async_computation.8 | async-start | bytes 8388608
  137.3 19.5 %slice-start.1 = ((s8[12582912]{0:T(1024)(128)(4,1)}), s8[4194304]{0:T(1024)(128)(4,1)S(1)}, s32[]{:S(2)}) async-start(s8[12582912]{0:T(1024)(128)(4,1)} %bitcast.114), calls=%async_computation.9 | async-start | bytes 8388608
  137.3 19.5 %slice-start.2 = ((s8[12582912]{0:T(1024)(128)(4,1)}), s8[4194304]{0:T(1024)(128)(4,1)S(1)}, s32[]{:S(2)}) async-start(s8[12582912]{0:T(1024)(128)(4,1)} %bitcast.114), calls=%async_computation.10 | async-start | bytes 8388608
  156.8 8.8 %copy-start.1 = (s32[8192,1]{1,0:T(8,128)S(1)}, s32[8192,1]{1,0:T(8,128)}, u32[]{:S(2)}) copy-start(s32[8192,1]{1,0:T(8,128)} %copy.101) | copy-start | bytes 98308
  289.0 7.6 copy-start.5
  291.8 7.0 copy-start.10
  291.8 24.8 %all-to-all-start = ((bf16[192,4,1024]{2,0,1:T(8,128)(2,1)}), bf16[192,4,1024]{2,0,1:T(8,128)(2,1)}, u32[]{:S(2)}, u32[]{:S(2)}) async-start(bf16[192,4,1024]{2,0,1:T(8,128)(2,1)} %bitcast.101), calls=%async_computation | async-start | bytes 3145728 | tf_op jit(solution)/shard_map/all_to_all | solution.py:574
  296.5 488.4 %reduce-scatter.5.cloned.1.call-start = ((), (), s32[]{:S(2)}) async-start(), calls=%async_computation.7 | async-start | bytes 10948608 | tf_op jit(solution)/shard_map/reduce_scatter | solution.py:605
  320.4 14.3 %copy-start.2 = (f32[1024,768]{0,1:T(8,128)}, f32[1024,768]{0,1:T(8,128)S(1)}, u32[]{:S(2)}) copy-start(f32[1024,768]{0,1:T(8,128)S(1)} %get-tuple-element.144) | copy-start | bytes 9437188
  334.8 11.1 %copy-start.8 = (bf16[3072,768]{1,0:T(8,128)(2,1)S(1)}, bf16[3072,768]{1,0:T(8,128)(2,1)}, u32[]{:S(2)}) copy-start(bf16[3072,768]{1,0:T(8,128)(2,1)} %reshape.415) | copy-start | bytes 14155780
  345.9 8.6 %copy-start = (bf16[1024,768]{0,1:T(8,128)(2,1)S(1)}, bf16[1024,768]{0,1:T(8,128)(2,1)}, u32[]{:S(2)}) copy-start(bf16[1024,768]{0,1:T(8,128)(2,1)} %copy.105) | copy-start | bytes 4718596
  367.0 15.4 %copy-start.3 = (f32[1024,768]{0,1:T(8,128)S(1)}, f32[1024,768]{0,1:T(8,128)}, u32[]{:S(2)}) copy-start(f32[1024,768]{0,1:T(8,128)} %copy-done.2) | copy-start | bytes 9437188
  397.9 11.9 %copy-start.4 = (f32[1024,768]{0,1:T(8,128)S(1)}, f32[1024,768]{0,1:T(8,128)}, u32[]{:S(2)}) copy-start(f32[1024,768]{0,1:T(8,128)} %copy-done.2) | copy-start | bytes 9437188
  427.5 372.9 %reduce-scatter.3.cloned.1.call-start = ((), (), s32[]{:S(2)}) async-start(), calls=%async_computation.6 | async-start | bytes 15728640 | tf_op jit(solution)/shard_map/reduce_scatter | solution.py:633
  494.6 147.3 %collective-permute-start = (bf16[384,2048]{1,0:T(8,128)(2,1)}, bf16[384,2048]{1,0:T(8,128)(2,1)}, u32[]{:S(2)}, u32[]{:S(2)}) collective-permute-start(bf16[384,2048]{1,0:T(8,128)(2,1)} %get-tuple-element.33), channel_id=1, source_target_pairs={{0,4},{1,5},{2,6},{3,7},{4,8},{5,9},{6,10},{7,11},{8,12},{9,13},{1... | collective-permute-start | bytes 4718600 | tf_op jit(solution)/shard_map/ppermute | solution.py:617
  511.5 130.5 %collective-permute-start.1 = (bf16[384,2048]{1,0:T(8,128)(2,1)}, bf16[384,2048]{1,0:T(8,128)(2,1)}, u32[]{:S(2)}, u32[]{:S(2)}) collective-permute-start(bf16[384,2048]{1,0:T(8,128)(2,1)} %get-tuple-element.34), channel_id=1, source_target_pairs={{4,0},{5,1},{6,2},{7,3},{8,4},{9,5},{10,6},{11,7},{12,8},{13,9},{1... | collective-permute-start | bytes 4718600 | tf_op jit(solution)/shard_map/ppermute | solution.py:616
  641.9 6.8 copy-start.11
  641.9 6.8 copy-start.13
  680.4 96.2 %all-to-all-start.2 = ((f32[32,24,576]{2,1,0:T(8,128)}), f32[32,24,576]{2,1,0:T(8,128)}, u32[]{:S(2)}, u32[]{:S(2)}) async-start(f32[32,24,576]{2,1,0:T(8,128)} %fusion.2), calls=%async_computation.3 | async-start | bytes 3932160 | tf_op jit(solution)/shard_map/all_to_all | solution.py:636
  (6 other events, 13.8 us)
Sparse Core Ops, SparseCore 0:
  10.9 132.4 all-gather.1
  427.6 216.2 reduce-scatter.4
  661.1 139.2 reduce-scatter.2
